TPU v7x, 128 devices: a whole 4x4x4 slice. The times are simulated.
128 devices in a mesh: row: 8 (over y, core), col: 16 (over z, x).
Axes of the slice: x: 4, y: 4, z: 4, core: 2. Of those that a mesh axis runs over, the one named last changes fastest.
Arguments:
- parent_front: float32 [8, 2048, 4, 4096], P(None, 'row', None, 'col'), may hold values from -6 to 6
- generators: bfloat16 [96, 256, 256], P('row'), may hold values from -1.5 to 1.5
- diagonal_blocks: bfloat16 [96, 256, 256], P('row'), may hold values from -6 to 6
- coupling: bfloat16 [2, 256, 256], replicated, may hold values from -0.375 to 0.375
- block_map: int32 [2, 48], replicated, may hold values from 0 to 63, as said below
- valid_rows: int32 [2, 48], replicated, may hold values from 128 to 256
Outputs:
- assembled: float32 [8, 2048, 4, 4096], P(None, 'row', None, 'col')
Inputs may be any that keep to these rules, and one draw needn't show every extreme that they name: `block_map`: for each child c and each s < 4, the child blocks s * 12 to (s + 1) * 12 - 1 map in increasing order to distinct parent blocks of the range s * 16 to (s + 1) * 16 - 1, and the parent blocks s * 16 + m * 8 of that range always receive one.
All inputs are finite; a program needn't handle non-finite values.
Results may differ from a plain program's by a relative error of at most 0.0028.
Values may be sent and summed in bfloat16 or wider, within the bound.
A program may use at most 128 MiB of HBM per device.

v0:
```python
import jax
import jax.numpy as jnp
from jax import lax
from jax.sharding import PartitionSpec as P


def sent_together(arrays, axis, dim, along):
    both = jnp.concatenate(arrays, axis=along)
    filled, at, outs = (lax.all_gather(both, axis, axis=dim, tiled=True), 0, [])
    for a in arrays:
        outs.append(lax.slice_in_dim(filled, at, at + a.shape[along], axis=along))
        at += a.shape[along]
    return tuple(outs)


def split_children(stacked, half_rows):
    grouped = stacked.reshape((half_rows, 2, -1) + stacked.shape[2:])
    grouped = jnp.swapaxes(grouped, 0, 1)
    return grouped.reshape((2, -1) + stacked.shape[2:])


def shards(parent_front, generators, diagonal_blocks, coupling, block_map, valid_rows):
    row_count = lax.axis_size("row")
    col_count = lax.axis_size("col")
    half_rows = row_count // 2
    row_index = lax.axis_index("row")
    col_index = lax.axis_index("col")
    own_child = row_index % 2
    own_group = row_index // 2
    group_blocks = generators.shape[0]
    block_size = generators.shape[1]
    rank_width = generators.shape[2]
    rows_local = parent_front.shape[0]
    cols_local = parent_front.shape[2]
    window = 2 * rows_local
    row_cap = window // row_count
    col_cap = window // col_count
    map_child = lax.dynamic_index_in_dim(block_map, own_child, 0, keepdims=False)
    count_child = lax.dynamic_index_in_dim(valid_rows, own_child, 0, keepdims=False)
    coupling_own = lax.dynamic_index_in_dim(coupling, own_child, 0, keepdims=False)
    group_start = own_group * group_blocks
    map_group = lax.dynamic_slice_in_dim(map_child, group_start, group_blocks)
    count_group = lax.dynamic_slice_in_dim(count_child, group_start, group_blocks)
    row_offsets = jnp.arange(block_size, dtype=jnp.int32)
    kept_mask = (row_offsets[None, :] < count_group[:, None]).astype(jnp.bfloat16)
    masked = generators * kept_mask[:, :, None]
    projected = jnp.einsum(
        "ixq,qr->ixr", masked, coupling_own, preferred_element_type=jnp.float32
    ).astype(jnp.bfloat16)
    diag_kept = diagonal_blocks * kept_mask[:, :, None] * kept_mask[:, None, :]
    window_pos = map_group - own_group * window
    slot_ids = jnp.arange(window, dtype=jnp.int32)
    window_place = (window_pos[None, :] == slot_ids[:, None]).astype(jnp.bfloat16)
    row_place = window_place.reshape(row_cap, row_count, group_blocks)
    row_send = jnp.einsum(
        "kri,ixq->rkxq", row_place, masked, preferred_element_type=jnp.float32
    ).astype(jnp.bfloat16)
    row_received = lax.all_to_all(row_send, "row", split_axis=0, concat_axis=0, tiled=True)
    row_received = split_children(row_received, half_rows)
    wanted = jnp.arange(col_cap, dtype=jnp.int32) * col_count + col_index
    column_pick = (window_pos[None, :] == wanted[:, None]).astype(jnp.bfloat16)
    col_send = jnp.einsum(
        "ki,izq->kzq", column_pick, projected, preferred_element_type=jnp.float32
    ).astype(jnp.bfloat16)
    diag_send = jnp.einsum(
        "ki,ixz->kxz", column_pick, diag_kept, preferred_element_type=jnp.float32
    ).astype(jnp.bfloat16)
    col_received, diag_received = sent_together((col_send, diag_send), "row", 0, 1)
    col_received = split_children(
        col_received.reshape(row_count, col_cap, block_size, rank_width), half_rows
    )
    diag_received = split_children(
        diag_received.reshape(row_count, col_cap, block_size, block_size), half_rows
    )
    row_parents = jnp.arange(rows_local, dtype=jnp.int32) * row_count + row_index
    col_parents = jnp.arange(cols_local, dtype=jnp.int32) * col_count + col_index
    on_diag = (row_parents[:, None] == col_parents[None, :]).astype(jnp.float32)
    running = parent_front
    for child_index in range(2):
        child_tile = jnp.einsum(
            "axq,bzq->axbz",
            row_received[child_index],
            col_received[child_index],
            preferred_element_type=jnp.float32,
        )
        diag_part = diag_received[child_index].astype(jnp.float32).transpose(1, 0, 2)
        child_tile = child_tile + on_diag[:, None, :, None] * diag_part[None]
        rounded = lax.optimization_barrier(child_tile.astype(jnp.bfloat16))
        running = running + rounded.astype(jnp.float32)
    return running


def solution(mesh):
    in_specs = (
        P(None, "row", None, "col"),
        P("row", None, None),
        P("row", None, None),
        P(),
        P(),
        P(),
    )
    out_specs = P(None, "row", None, "col")
    return jax.shard_map(shards, mesh=mesh, in_specs=in_specs, out_specs=out_specs, check_vma=False)
```

profile of v0, /device:TPU:0, one launch (start us, length us, event | category | flops | bytes accessed | tf_op | source)
XLA Modules:
  0.0 94.3 jit_solution(12038976815060474854)
XLA Ops:
  6.5 0.9 dynamic-slice_bitcast_fusion
  7.5 0.1 fusion.15
  7.5 2.1 %convolution_convert_fusion = bf16[12,256,256]{2,1,0:T(8,128)(2,1)S(1)} fusion(bf16[12,256,256]{2,1,0:T(8,128)(2,1)} %param.7, bf16[12,256]{1,0:T(8,128)(2,1)S(1)} %fusion.15, bf16[2,256,256]{2,1,0:T(8,128)(2,1)S(1)} %copy-done, s32[]{:T(128)S(6)} %select_n.27), kind=kOutput, calls=%fused_computation.12 | convolution fusion | flops 404226048 | bytes 3284996 | tf_op jit(solution)/shard_map/ixq,qr->ixr/dot_general | solution.py:47
  9.6 0.6 multiply_bitcast_fusion
  10.3 0.1 copy-done.3
  10.3 1.0 %fusion.5 = bf16[1,256,256]{2,0,1:T(2,128)(2,1)S(1)} fusion(bf16[12,256,256]{2,1,0:T(8,128)(2,1)S(1)} %convolution_convert_fusion, s32[]{:T(128)S(6)} %axis_index.25, s32[2,48]{1,0:T(2,128)S(1)} %copy-done.3, s32[]{:T(128)S(6)} %select_n.28, s32[]{:T(128)S(6)} %select_n.31, s32[]{:T(128)S(6)} %mul.69), kind=kOutput, calls=%fused_computation.8 | convolution fusion | flops 1572888 | bytes 1704464 | tf_op jit(solution)/shard_map/ki,izq->kzq/dot_general | solution.py:62
  11.3 1.0 %fusion.3 = bf16[1,256,256]{2,0,1:T(2,128)(2,1)S(1)} fusion(bf16[12,256,256]{2,1,0:T(8,128)(2,1)S(1)} %get-tuple-element.12, s32[]{:T(128)S(6)} %axis_index.25, s32[2,48]{1,0:T(2,128)S(1)} %copy-done.3, s32[]{:T(128)S(6)} %select_n.28, s32[]{:T(128)S(6)} %select_n.31, s32[]{:T(128)S(6)} %mul.69), kind=kOutput, calls=%fused_computation.6 | convolution fusion | flops 1572888 | bytes 1704464 | tf_op jit(solution)/shard_map/ki,ixz->kxz/dot_general | solution.py:65
  12.4 0.7 pad_maximum_fusion
  13.2 0.1 fusion.31
  13.3 1.1 %convert_bitcast_fusion = bf16[8,2,256,256]{3,0,1,2:T(8,128)(2,1)S(1)} fusion(bf16[12,256,256,1]{2,1,0,3:T(8,128)(2,1)S(1)} %get-tuple-element.11, s32[2,8]{1,0:T(2,128)S(1)} %multiply_add_fusion, s32[12]{0:T(128)S(1)} %fusion.31), kind=kOutput, calls=%fused_computation.11 | convolution fusion | flops 26214592 | bytes 3670128 | tf_op jit(solution)/shard_map/kri,ixq->rkxq/dot_general | solution.py:55
  14.4 2.9 %copy.19 = bf16[8,2,256,256]{3,1,2,0:T(2,128)(2,1)} copy(bf16[8,2,256,256]{3,0,1,2:T(8,128)(2,1)S(1)} %convert_bitcast_fusion) | data formatting | bytes 4194304 | tf_op jit(solution)/shard_map/convert_element_type | solution.py:57
  17.4 4.6 %all-to-all-start = ((bf16[8,2,256,256]{3,1,2,0:T(2,128)(2,1)}), bf16[8,2,256,256]{3,1,2,0:T(2,128)(2,1)S(1)}, u32[]{:S(2)}, u32[]{:S(2)}) async-start(bf16[8,2,256,256]{3,1,2,0:T(2,128)(2,1)} %copy.19), calls=%async_computation | async-start | bytes 4194304 | tf_op jit(solution)/shard_map/all_to_all | solution.py:58
  22.0 0.1 compare_convert_fusion
  22.0 35.5 %all-to-all-done = bf16[8,2,256,256]{3,1,2,0:T(2,128)(2,1)S(1)} async-done(((bf16[8,2,256,256]{3,1,2,0:T(2,128)(2,1)}), bf16[8,2,256,256]{3,1,2,0:T(2,128)(2,1)S(1)}, u32[]{:S(2)}, u32[]{:S(2)}) %all-to-all-start) | async-done | bytes 2097184 | tf_op jit(solution)/shard_map/all_to_all | solution.py:58
  57.5 0.3 copy.52
  57.9 0.1 fusion.27
  58.0 0.0 all-gather.2.cloned.1.call-done
  58.0 1.7 %fusion.28 = (bf16[8,256,256]{2,1,0:T(8,128)(2,1)S(1)}, bf16[8,256,256]{2,1,0:T(8,128)(2,1)S(1)}) fusion(bf16[8,512,256]{2,1,0:T(8,128)(2,1)} %all-gather.2.cloned.1.call-done), kind=kLoop, calls=%fused_computation.51 | loop fusion | bytes 4194304 | tf_op jit(solution)/shard_map/slice | solution.py:11
  59.7 0.1 copy.53
  59.8 0.2 convert_bitcast_fusion.2
  60.0 1.4 %add_convert_fusion.1 = bf16[8,256,4,256]{3,1,2,0:T(8,128)(2,1)S(1)} fusion(f32[256,4,256]{2,0,1:T(8,128)S(1)} %get-tuple-element.9, f32[8,4]{1,0:T(8,128)S(1)} %compare_convert_fusion, bf16[8,256,256,1]{2,1,3,0:T(8,128)(2,1)S(1)} %bitcast.89, bf16[2,4,1,256,256]{4,3,1,2,0:T(8,128)(2,1)S(1)} %bitcast.86), kind=kOutput, calls=%fused_computation.3 | convolution fusion | flops 1080033280 | bytes 6819840 | tf_op jit(solution)/shard_map/axq,bzq->axbz/dot_general | solution.py:80
  61.4 3.4 %add_convert_fusion = bf16[8,256,4,256]{3,1,2,0:T(8,128)(2,1)} fusion(f32[256,4,256]{2,0,1:T(8,128)S(1)} %get-tuple-element.10, f32[8,4]{1,0:T(8,128)S(1)} %compare_convert_fusion, bf16[8,256,256,1]{2,1,3,0:T(8,128)(2,1)S(1)} %bitcast.88, bf16[2,4,1,256,256]{4,3,1,2,0:T(8,128)(2,1)S(1)} %bitcast.87), kind=kOutput, calls=%fused_computation.2 | convolution fusion | flops 1080033280 | bytes 6819840 | tf_op jit(solution)/shard_map/axq,bzq->axbz/dot_general | solution.py:80
  64.9 10.5 %fusion = f32[8,256,4,256]{3,1,2,0:T(8,128)} fusion(f32[8,256,4,256]{3,2,1,0:T(4,128)} %param.6, bf16[8,256,4,256]{3,1,2,0:T(8,128)(2,1)} %add_convert_fusion, bf16[8,256,4,256]{3,1,2,0:T(8,128)(2,1)S(1)} %add_convert_fusion.1), kind=kLoop, calls=%fused_computation.1 | loop fusion | flops 8388608 | bytes 25165824 | tf_op jit(solution)/shard_map/add | solution.py:89
  75.3 12.2 %copy.23 = f32[8,256,4,256]{3,2,1,0:T(4,128)} copy(f32[8,256,4,256]{3,1,2,0:T(8,128)} %fusion) | data formatting | bytes 16777216 | tf_op jit(solution)/shard_map/add | solution.py:89
  (13 shorter events, 0.1 us)
Async XLA Ops:
  6.5 1.0 %copy-start = (bf16[2,256,256]{2,1,0:T(8,128)(2,1)S(1)}, bf16[2,256,256]{2,1,0:T(8,128)(2,1)}, u32[]{:S(2)}) copy-start(bf16[2,256,256]{2,1,0:T(8,128)(2,1)} %param.9) | copy-start | bytes 786436
  6.5 3.1 %copy-start.1 = (bf16[12,256,256]{2,1,0:T(8,128)(2,1)S(1)}, bf16[12,256,256]{2,1,0:T(8,128)(2,1)}, u32[]{:S(2)}) copy-start(bf16[12,256,256]{2,1,0:T(8,128)(2,1)} %param.7) | copy-start | bytes 4718596
  6.5 51.5 %all-gather.2.cloned.1.call-start = ((), (), s32[]{:S(2)}) async-start(), calls=%async_computation.1 | async-start | bytes 2359296 | tf_op jit(solution)/shard_map/all_gather | solution.py:9
  6.5 3.1 %copy-start.2 = (bf16[12,256,256]{2,1,0:T(8,128)(2,1)S(1)}, bf16[12,256,256]{2,1,0:T(8,128)(2,1)}, u32[]{:S(2)}) copy-start(bf16[12,256,256]{2,1,0:T(8,128)(2,1)} %param.8) | copy-start | bytes 4718596
  9.6 0.7 copy-start.3
  17.4 40.2 %all-to-all-start = ((bf16[8,2,256,256]{3,1,2,0:T(2,128)(2,1)}), bf16[8,2,256,256]{3,1,2,0:T(2,128)(2,1)S(1)}, u32[]{:S(2)}, u32[]{:S(2)}) async-start(bf16[8,2,256,256]{3,1,2,0:T(2,128)(2,1)} %copy.19), calls=%async_computation | async-start | bytes 4194304 | tf_op jit(solution)/shard_map/all_to_all | solution.py:58
Sparse Core Ops, SparseCore 0:
  13.3 35.9 all-gather.1
where the time goes:
time: 95 us; the launch traced here: 94.3 us
  waiting for transfers between devices  35.5 us (37%)
  local copies, waits for them, and re-layouts  18.4 us (19%)
  between operations  13.5 us (14%)
  other arithmetic  12.2 us (13%)
  matrix products  10.1 us (11%)
  starting transfers between devices  4.58 us (5%)
    all_to_all x1, waiting for transfers between devices, shards(): lax.all_to_all(row_send, 'row', split_axis=0, concat_axis=0, tiled=True)  35.5 us
    add x1, local copies, waits for them, and re-layouts, shards(): running = running + rounded.astype(jnp.float32)  12.2 us
    add x1, other arithmetic, shards(): running = running + rounded.astype(jnp.float32)  10.5 us
    dot_general x2, matrix products, shards(): jnp.einsum('axq,bzq->axbz', row_received[child_index], col_received[child...  4.84 us
    all_to_all x1, starting transfers between devices, shards(): lax.all_to_all(row_send, 'row', split_axis=0, concat_axis=0, tiled=True)  4.58 us
    convert_element_type x1, local copies, waits for them, and re-layouts, shards(): row_send = jnp.einsum('kri,ixq->rkxq', row_place, masked, preferred_eleme...  2.94 us
    dot_general x1, matrix products, shards(): jnp.einsum('ixq,qr->ixr', masked, coupling_own, preferred_element_type=jn...  2.07 us
  transfers between devices with their start and end apart: 2, of which 1 were waited for; matrix products, arithmetic and copies ran while one was open for 5% of the time, Pallas kernels for 0%

commit v1 on v0

v1 whole, which is shorter than its diff:
```python
import jax
import jax.numpy as jnp
from jax import lax
from jax.experimental import pallas as pl
from jax.experimental.pallas import tpu as pltpu
from jax.sharding import PartitionSpec as P

MESH = pl.DeviceIdType.MESH
CHIPS = 4
CORES = 2
SIDE = 4
GROUP = 12
WINDOW = 16
STRIPS = 16
BLK = 256
STRIP = BLK // STRIPS
UNITS = 2 * CHIPS
LANES = 128
HALF = BLK // 2


def semaphore_table():
    names = []
    for h in range(2):
        names += [("A1", h, d) for d in (1, -1)]
        names += [("A2", h, d) for d in (1, -1)]
        names += [("B1", h, i, d) for i in ("own", 1, -1, 2, -2) for d in (1, -1)]
        names += [("B2", h, i, 1) for i in ("own", 1, -1, 2)]
        names += [("B2", h, i, -1) for i in ("own", 1, -1, -2)]
    names += [("S", i) for i in range(6)]
    names += [("PR",)]
    for part in range(2):
        names += [("CP", part)]
        for d in (1, -1):
            names += [("C", part, d), ("CF", part, d), ("CN", part, d), ("CQ", part, d)]
    return {name: i for i, name in enumerate(names)}


SEMS = semaphore_table()


def gather_kernel(bmap, gen, diag, parent, g, cd, front, gp, gv, dv, sb, pb, lsem, ssem, rsem):
    r = lax.axis_index("row")
    t = lax.axis_index("col")
    y, c = r // CORES, r % CORES
    z, x = t // SIDE, t % SIDE
    partner = (y * CORES + 1 - c, t)

    def wrap(v):
        return (v + 8) % 4

    def ydev(step, core):
        return (wrap(y + step) * CORES + core, t)

    load_strip = pltpu.make_async_copy(gen.at[:, pl.ds(t * STRIP, STRIP), :], gp, lsem.at[0])
    load_gen = pltpu.make_async_copy(gen, gv, lsem.at[1])
    load_diag = pltpu.make_async_copy(diag, dv, lsem.at[2])
    load_front = pltpu.make_async_copy(parent, front, lsem.at[3])
    load_strip.start()
    load_gen.start()
    load_diag.start()
    load_front.start()

    barrier = pltpu.get_barrier_semaphore()
    peers = [ydev(s, k) for s in (1, 2, 3) for k in range(CORES)] + [partner]
    for s in (1, -1):
        peers += [(r, z * SIDE + wrap(x + s)), (r, wrap(z + s) * SIDE + x)]
    for peer in peers:
        pl.semaphore_signal(barrier, inc=1, device_id=peer, device_id_type=MESH)

    entries = [bmap[c, y * GROUP + i] for i in range(GROUP)]

    def source(slot):
        at = y * WINDOW + slot
        before = jnp.int32(0)
        for e in entries:
            before = before + jnp.where(e < at, 1, 0).astype(jnp.int32)
        return jnp.minimum(before, GROUP - 1)

    load_strip.wait()
    for d in (1, 2, 3):
        for k in range(CORES):
            for m in range(2):
                slot = m * 8 + CORES * wrap(y - d) + k
                sb[(d - 1) * CORES + k, m] = gp[source(slot)]
    load_gen.wait()
    cd[c, y, 0] = gv[source(t)]
    for m in range(2):
        g[c, :, m] = gv[source(m * 8 + r)].reshape(STRIPS, STRIP, BLK)
        pb[:, m] = gv[source(m * 8 + y * CORES + 1 - c)].reshape(STRIPS, STRIP, BLK)
    load_diag.wait()
    cd[c, y, 1] = dv[source(t)]

    pl.semaphore_wait(barrier, len(peers))

    sent = []

    def send(name, src, dst, to, recv=None):
        k = SEMS[name]
        copy = pltpu.make_async_remote_copy(
            src_ref=src, dst_ref=dst, send_sem=ssem.at[k], recv_sem=rsem.at[k if recv is None else recv],
            device_id=to, device_id_type=MESH,
        )
        copy.start()
        sent.append(copy)

    def arrived(name, ref):
        k = SEMS[name]
        pltpu.make_async_remote_copy(
            src_ref=ref, dst_ref=ref, send_sem=ssem.at[k], recv_sem=rsem.at[k],
            device_id=partner, device_id_type=MESH,
        ).wait_recv()

    for d in (2, 1, 3):
        for k in range(CORES):
            i = (d - 1) * CORES + k
            send(("S", i), sb.at[i], g.at[c, t, pl.ds(2 * d, 2)], ydev(-d, k), SEMS[("S", 0)] + (d - 1) * CORES + c)
    for part in range(2):
        for d in (1, -1):
            send(("C", part, d), cd.at[c, y, part], cd.at[c, y, part], ydev(d, c))
    send(("PR",), pb, g.at[c, :, pl.ds(0, 2)], partner)
    for part in range(2):
        send(("CP", part), cd.at[c, y, part], cd.at[c, y, part], partner)

    pos = [(x, z), (z, x)]

    def dev(h, dp, dq):
        p, q = wrap(pos[h][0] + dp), wrap(pos[h][1] + dq)
        return (r, q * SIDE + p) if h == 0 else (r, p * SIDE + q)

    def piece(h, dp, dq, part=None):
        at = dev(h, dp, dq)[1]
        if part is None:
            return g.at[h, at, pl.ds(2, 6)]
        return g.at[h, at, pl.ds(2 + 3 * part, 3)]

    def item_ref(h, item, dq):
        if item == "own":
            return piece(h, 0, dq)
        if item in (1, -1):
            return piece(h, item, dq)
        return piece(h, 2, dq, 0 if item == 2 else 1)

    def half_ref(h, item, dq, part):
        if item == "own":
            return piece(h, 0, dq, part)
        if item in (1, -1):
            return piece(h, item, dq, part)
        return piece(h, 2, dq, part)

    def first_q(h, item):
        for d in (1, -1):
            ref = item_ref(h, item, 0)
            send(("B1", h, item, d), ref, ref, dev(h, 0, d))

    def second_q(h, item):
        for d in (1, -1):
            part = 0 if d == 1 else 1
            if item not in (2, -2):
                arrived(("B1", h, item, d), item_ref(h, item, -d))
                ref = half_ref(h, item, -d, part)
                send(("B2", h, item, d), ref, ref, dev(h, 0, d))

    def second_q_far(h):
        for d in (1, -1):
            for item in (2, -2):
                arrived(("B1", h, item, d), item_ref(h, item, -d))
        for d in (1, -1):
            item = 2 * d
            ref = item_ref(h, item, -d)
            send(("B2", h, item, d), ref, ref, dev(h, 0, d))

    for h in range(2):
        for d in (1, 2, 3):
            arrived(("S", (d - 1) * CORES + h), g.at[h, t, pl.ds(2 * d, 2)])
    for h in range(2):
        for d in (1, -1):
            ref = piece(h, 0, 0)
            send(("A1", h, d), ref, ref, dev(h, d, 0))
    for h in range(2):
        first_q(h, "own")

    def near(part):
        for d in (1, -1):
            ref = cd.at[c, wrap(y - d), part]
            arrived(("C", part, d), ref)
            half = cd.at[c, wrap(y - d), part, pl.ds(0 if d == 1 else HALF, HALF)]
            send(("CF", part, d), half, half, ydev(d, c))
            send(("CN", part, d), ref, ref, partner)

    def far(part):
        for d in (1, -1):
            half = cd.at[c, wrap(y + 2), part, pl.ds(0 if d == 1 else HALF, HALF)]
            arrived(("CF", part, d), half)
            send(("CQ", part, d), half, half, partner)

    near(0)
    for h in range(2):
        for d in (1, -1):
            arrived(("A1", h, d), piece(h, -d, 0))
            ref = piece(h, -d, 0, 0 if d == 1 else 1)
            send(("A2", h, d), ref, ref, dev(h, d, 0))
        for d in (1, -1):
            first_q(h, -d)
    for h in range(2):
        second_q(h, "own")
    for h in range(2):
        for d in (1, -1):
            arrived(("A2", h, d), piece(h, 2, 0, 0 if d == 1 else 1))
            first_q(h, 2 * d)
    near(1)
    far(0)
    for h in range(2):
        for d in (1, -1):
            second_q(h, d)
    for h in range(2):
        second_q_far(h)
    far(1)

    for h in range(2):
        for d in (1, -1):
            part = 0 if d == 1 else 1
            for item in ("own", 1, -1, 2 * d):
                arrived(("B2", h, item, d), half_ref(h, item, 2, part))
    other = 1 - c
    arrived(("PR",), g.at[other, :, pl.ds(0, 2)])
    for part in range(2):
        arrived(("CP", part), cd.at[other, y, part])
        for d in (1, -1):
            arrived(("CN", part, d), cd.at[other, wrap(y - d), part])
            arrived(("CQ", part, d), cd.at[other, wrap(y + 2), part, pl.ds(0 if d == 1 else HALF, HALF)])
    load_front.wait()
    for copy in sent:
        copy.wait_send()


def tile_kernel(bmap, vrows, g, cd, coup, front, out, pscr, ascr):
    r = lax.axis_index("row")
    t = lax.axis_index("col")
    y = r // CORES
    a = pl.program_id(0)

    def kept(child, group, parent_block):
        total = jnp.int32(0)
        for i in range(GROUP):
            at = group * GROUP + i
            total = total + jnp.where(bmap[child, at] == parent_block, vrows[child, at], 0)
        return total

    rows = lax.broadcasted_iota(jnp.int32, (BLK, BLK), 0)

    @pl.when(a == 0)
    def _():
        for s in range(CHIPS):
            for child in range(2):
                count = kept(child, s, s * WINDOW + t)
                col = jnp.where(rows < count, cd[child, s, 0], jnp.zeros((BLK, BLK), jnp.bfloat16))
                proj = jnp.dot(col, coup[child], preferred_element_type=jnp.float32)
                pscr[s, :, child * BLK:(child + 1) * BLK] = proj.astype(jnp.bfloat16)

    s, m = a // 2, a % 2
    away = (s - y + CHIPS) % CHIPS
    for child in range(2):
        count = kept(child, s, a * 8 + r)
        block = g[child, :, 2 * away + m].reshape(BLK, BLK)
        ascr[:, child * BLK:(child + 1) * BLK] = jnp.where(rows < count, block, jnp.zeros((BLK, BLK), jnp.bfloat16))
    dst = out.at[0]
    src = front.at[a]
    for b in range(CHIPS):
        tile = lax.dot_general(
            ascr[...], pscr[b], (((1,), (1,)), ((), ())), preferred_element_type=jnp.float32
        )
        for side in range(2):
            at = pl.ds(side * CHIPS + b, BLK, stride=8)
            dst[at, :] = src[at, :] + tile[:, side * LANES:(side + 1) * LANES]

    @pl.when(jnp.logical_and(r == t % 8, m == t // 8))
    def _():
        cols = lax.broadcasted_iota(jnp.int32, (BLK, LANES), 1)
        down = lax.broadcasted_iota(jnp.int32, (BLK, LANES), 0)
        for side in range(2):
            at = pl.ds(side * CHIPS + s, BLK, stride=8)
            total = dst[at, :]
            for child in range(2):
                count = kept(child, s, a * 8 + r)
                inside = jnp.logical_and(down < count, cols + side * LANES < count)
                part = cd[child, s, 1, :, side * LANES:(side + 1) * LANES].astype(jnp.float32)
                total = total + jnp.where(inside, part, 0.0)
            dst[at, :] = total


def shards(parent_front, generators, diagonal_blocks, coupling, block_map, valid_rows):
    flat = parent_front.reshape(8, BLK, CHIPS, 2, LANES).transpose(0, 1, 3, 2, 4).reshape(8, BLK * 8, LANES)
    any_spec = pl.BlockSpec(memory_space=pl.ANY)
    vmem = pl.BlockSpec(memory_space=pltpu.VMEM)
    smem = pl.BlockSpec(memory_space=pltpu.SMEM)
    bf16 = jnp.bfloat16
    g, cd, front = pl.pallas_call(
        gather_kernel,
        name="gather",
        in_specs=[smem, any_spec, any_spec, any_spec],
        out_specs=[vmem, vmem, vmem],
        out_shape=[
            pltpu.VMEM((2, STRIPS, UNITS, STRIP, BLK), bf16),
            pltpu.VMEM((2, CHIPS, 2, BLK, BLK), bf16),
            pltpu.VMEM((8, BLK * 8, LANES), jnp.float32),
        ],
        scratch_shapes=[
            pltpu.VMEM((GROUP, STRIP, BLK), bf16),
            pltpu.VMEM((GROUP, BLK, BLK), bf16),
            pltpu.VMEM((GROUP, BLK, BLK), bf16),
            pltpu.VMEM((6, 2, STRIP, BLK), bf16),
            pltpu.VMEM((STRIPS, 2, STRIP, BLK), bf16),
            pltpu.SemaphoreType.DMA((4,)),
            pltpu.SemaphoreType.DMA((len(SEMS),)),
            pltpu.SemaphoreType.DMA((len(SEMS),)),
        ],
        compiler_params=pltpu.CompilerParams(
            collective_id=0, has_side_effects=True, vmem_limit_bytes=48 << 20
        ),
    )(block_map, generators, diagonal_blocks, flat)
    out = pl.pallas_call(
        tile_kernel,
        name="tiles",
        grid=(8,),
        in_specs=[smem, smem, vmem, vmem, vmem, vmem],
        out_specs=pl.BlockSpec((1, BLK * 8, LANES), lambda a: (a, 0, 0)),
        out_shape=jax.ShapeDtypeStruct((8, BLK * 8, LANES), jnp.float32),
        scratch_shapes=[
            pltpu.VMEM((CHIPS, BLK, 2 * BLK), bf16),
            pltpu.VMEM((BLK, 2 * BLK), bf16),
        ],
        compiler_params=pltpu.CompilerParams(vmem_limit_bytes=40 << 20),
    )(block_map, valid_rows, g, cd, coupling, front)
    return out.reshape(8, BLK, 2, CHIPS, LANES).transpose(0, 1, 3, 2, 4).reshape(8, BLK, CHIPS, BLK)


def solution(mesh):
    in_specs = (
        P(None, "row", None, "col"),
        P("row", None, None),
        P("row", None, None),
        P(),
        P(),
        P(),
    )
    out_specs = P(None, "row", None, "col")
    return jax.shard_map(shards, mesh=mesh, in_specs=in_specs, out_specs=out_specs, check_vma=False)
```

time: 95 us -> 38.8 us (0.41)
  Pallas kernels: 0 us -> 38.6 us
  waiting for transfers between devices: 35.5 us -> 0 us
  local copies, waits for them, and re-layouts: 18.4 us -> 0.01 us
  between operations: 13.5 us -> 0.03 us
  other arithmetic: 12.2 us -> 0 us
  matrix products: 10.1 us -> 0 us
  starting transfers between devices: 4.58 us -> 0 us
    pallas_call x0 -> x2, Pallas kernels: none -> 38.6 us  [the longest x1 29.9 us: shards(): pl.pallas_call(gather_kernel, name='gather', in_specs=[smem, any_spec, an...]
    all_to_all x1 -> x0, waiting for transfers between devices: 35.5 us -> none  [shards(): lax.all_to_all(row_send, 'row', split_axis=0, concat_axis=0, tiled=True)]
    add x1 -> x0, local copies, waits for them, and re-layouts: 12.2 us -> none  [shards(): running = running + rounded.astype(jnp.float32)]
    add x3 -> x0, other arithmetic: 10.5 us -> none  [the longest x1 10.5 us: shards(): running = running + rounded.astype(jnp.float32)]
    dot_general x6 -> x0, matrix products: 10.1 us -> none  [the longest x2 4.84 us: shards(): jnp.einsum('axq,bzq->axbz', row_received[child_index], col_received[child...]
    all_to_all x1 -> x0, starting transfers between devices: 4.58 us -> none  [shards(): lax.all_to_all(row_send, 'row', split_axis=0, concat_axis=0, tiled=True)]
    convert_element_type x2 -> x0, local copies, waits for them, and re-layouts: 2.98 us -> none  [the longest x1 2.94 us: shards(): row_send = jnp.einsum('kri,ixq->rkxq', row_place, masked, preferred_eleme...]
    slice x2 -> x0, local copies, waits for them, and re-layouts: 1.82 us -> none  [the longest x1 1.68 us: sent_together(): outs.append(lax.slice_in_dim(filled, at, at + a.shape[along], axis=along))]
  transfers between devices with their start and end apart: 2 -> 0, of which waited for: 1 -> 0; matrix products, arithmetic and copies ran while one was open for 5% -> 0% of each run, Pallas kernels for 0% -> 0%
where the time goes in v1:
time: 38.8 us; the launch traced here: 38.7 us
  Pallas kernels  38.6 us (99%)
    pallas_call x1, Pallas kernels, shards(): pl.pallas_call(gather_kernel, name='gather', in_specs=[smem, any_spec, an...  29.9 us
    pallas_call x1, Pallas kernels, shards(): pl.pallas_call(tile_kernel, name='tiles', grid=(8,), in_specs=[smem, smem...  8.68 us

profile of v1, /device:TPU:0, one launch (start us, length us, event | category | flops | bytes accessed | tf_op | source)
XLA Modules:
  0.0 38.7 jit_solution(14996867074194245519)
XLA Ops:
  0.0 0.0 copy-start
  0.0 0.0 copy-start.1
  0.0 0.0 copy-start.2
  0.0 29.9 %gather.1 = (bf16[2,16,8,16,256]{4,3,2,1,0:T(8,128)(2,1)S(1)}, bf16[2,4,2,256,256]{4,3,2,1,0:T(8,128)(2,1)S(1)}, f32[8,2048,128]{2,1,0:T(8,128)S(1)}) custom-call(s32[2,48]{1,0:T(2,128)} %bmap.3, bf16[12,256,256]{2,1,0:T(8,128)(2,1)} %gen.1, bf16[12,256,256]{2,1,0:T(8,128)(2,1)} %diag.1, f32[8,2048,128]{2,1,0:T(8,128)} %bitcast.10), custom_call_target="tpu_custom_call" | custom-call | tf_op jit(solution)/shard_map/gather/pallas_call | solution.py:298
  29.9 0.0 copy-done
  29.9 0.0 copy-done.1
  30.0 0.0 copy-done.2
  30.0 8.7 %tiles.1 = f32[8,2048,128]{2,1,0:T(8,128)} custom-call(s32[2,48]{1,0:T(2,128)S(1)} %copy-done.1, s32[2,48]{1,0:T(2,128)S(1)} %copy-done.2, bf16[2,16,8,16,256]{4,3,2,1,0:T(8,128)(2,1)S(1)} %get-tuple-element.8.g, bf16[2,4,2,256,256]{4,3,2,1,0:T(8,128)(2,1)S(1)} %get-tuple-element.9.cd, bf16[2,256,256]{2,1,0:T(8,128)(2,1)S(1)} %copy-done, ...), custom_call_target="tpu_custom_call" | custom-call | tf_op jit(solution)/shard_map/tiles/pallas_call | solution.py:322
Async XLA Ops:
  0.0 29.9 %copy-start = (bf16[2,256,256]{2,1,0:T(8,128)(2,1)S(1)}, bf16[2,256,256]{2,1,0:T(8,128)(2,1)}, u32[]{:S(2)}) copy-start(bf16[2,256,256]{2,1,0:T(8,128)(2,1)} %coup.1) | copy-start | bytes 786436
  0.0 29.9 %copy-start.1 = (s32[2,48]{1,0:T(2,128)S(1)}, s32[2,48]{1,0:T(2,128)}, u32[]{:S(2)}) copy-start(s32[2,48]{1,0:T(2,128)} %bmap.3) | copy-start | bytes 1156
  0.0 30.0 %copy-start.2 = (s32[2,48]{1,0:T(2,128)S(1)}, s32[2,48]{1,0:T(2,128)}, u32[]{:S(2)}) copy-start(s32[2,48]{1,0:T(2,128)} %vrows.1) | copy-start | bytes 1156

commit v2 on v0

v2 whole, which is shorter than its diff:
```python
import jax
import jax.numpy as jnp
from jax import lax
from jax.experimental import pallas as pl
from jax.experimental.pallas import tpu as pltpu
from jax.sharding import PartitionSpec as P

MESH = pl.DeviceIdType.MESH
CHIPS = 4
CORES = 2
SIDE = 4
GROUP = 12
WINDOW = 16
STRIPS = 16
BLK = 256
STRIP = BLK // STRIPS
UNITS = 2 * CHIPS
LANES = 128
HALF = BLK // 2


def semaphore_table():
    names = []
    for m in range(2):
        names += [("A1", m, d) for d in (1, -1)]
        names += [("A2", m, d) for d in (1, -1)]
        names += [("B1", m, i, d) for i in ("own", 1, -1, 2, -2) for d in (1, -1)]
        names += [("B2", m, i, 1) for i in ("own", 1, -1, 2)]
        names += [("B2", m, i, -1) for i in ("own", 1, -1, -2)]
        names += [("S", m, i) for i in range(6)]
        names += [("PR", m)]
    for part in range(2):
        names += [("CP", part)]
        for d in (1, -1):
            names += [("C", part, d, k) for k in range(2)]
            names += [("CF", part, d), ("CN", part, d), ("CQ", part, d)]
    return {name: i for i, name in enumerate(names)}


SEMS = semaphore_table()


def gather_kernel(
    bmap, vrows, gen, diag, coup, parent, front, g, cd, gp, gv, dv, cw, sb, pb, pt, ascr, lsem, ssem, rsem
):
    r = lax.axis_index("row")
    t = lax.axis_index("col")
    y, c = r // CORES, r % CORES
    z, x = t // SIDE, t % SIDE
    other = 1 - c
    partner = (y * CORES + other, t)
    pos = [(x, z), (z, x)]

    def wrap(v):
        return (v + 8) % 4

    def ydev(step, core):
        return (wrap(y + step) * CORES + core, t)

    def dev(m, dp, dq):
        p, q = wrap(pos[m][0] + dp), wrap(pos[m][1] + dq)
        return (r, q * SIDE + p) if m == 0 else (r, p * SIDE + q)

    def strip(m, dp, dq):
        return wrap(pos[m][1] + dq) * SIDE + wrap(pos[m][0] + dp)

    load_strips = [
        pltpu.make_async_copy(gen.at[:, pl.ds(strip(m, 0, 0) * STRIP, STRIP), :], gp.at[m], lsem.at[m])
        for m in range(2)
    ]
    load_gen = pltpu.make_async_copy(gen, gv, lsem.at[2])
    load_diag = pltpu.make_async_copy(diag, dv, lsem.at[3])
    load_coup = pltpu.make_async_copy(coup, cw, lsem.at[4])
    load_front = pltpu.make_async_copy(parent, front, lsem.at[5])
    for load in load_strips:
        load.start()

    barrier = pltpu.get_barrier_semaphore()
    peers = [ydev(s, k) for s in (1, 2, 3) for k in range(CORES)] + [partner]
    peers += [dev(0, s, 0) for s in (1, -1)] + [dev(1, s, 0) for s in (1, -1)]
    for peer in peers:
        pl.semaphore_signal(barrier, inc=1, device_id=peer, device_id_type=MESH)
    load_gen.start()
    load_diag.start()
    load_coup.start()

    entries = [bmap[c, y * GROUP + i] for i in range(GROUP)]

    def source(slot):
        at = y * WINDOW + slot
        before = jnp.int32(0)
        for e in entries:
            before = before + jnp.where(e < at, 1, 0).astype(jnp.int32)
        return jnp.minimum(before, GROUP - 1)

    def kept(child, group, parent_block):
        total = jnp.int32(0)
        for i in range(GROUP):
            at = group * GROUP + i
            total = total + jnp.where(bmap[child, at] == parent_block, vrows[child, at], 0)
        return total

    for load in load_strips:
        load.wait()
    for m in range(2):
        for d in (2, 1, 3):
            for k in range(CORES):
                sb[m, (d - 1) * CORES + k] = gp[m, source(m * 8 + CORES * wrap(y - d) + k)]

    pl.semaphore_wait(barrier, len(peers))

    sent = []

    def send(name, src, dst, to, recv=None):
        k = SEMS[name]
        copy = pltpu.make_async_remote_copy(
            src_ref=src, dst_ref=dst, send_sem=ssem.at[k], recv_sem=rsem.at[k if recv is None else recv],
            device_id=to, device_id_type=MESH,
        )
        copy.start()
        sent.append(copy)

    def arrived(name, ref):
        k = SEMS[name]
        pltpu.make_async_remote_copy(
            src_ref=ref, dst_ref=ref, send_sem=ssem.at[k], recv_sem=rsem.at[k],
            device_id=partner, device_id_type=MESH,
        ).wait_recv()

    for d in (2, 1, 3):
        for m in range(2):
            for k in range(CORES):
                i = (d - 1) * CORES + k
                send(
                    ("S", m, i), sb.at[m, i], g.at[m, strip(m, 0, 0), 2 * d + c],
                    ydev(-d, k), SEMS[("S", m, 0)] + (d - 1) * CORES + c,
                )
    load_gen.wait()
    cd[c, y, 0] = gv[source(t)]
    for m in range(2):
        pb[m] = gv[source(m * 8 + y * CORES + other)].reshape(STRIPS, STRIP, BLK)

    def rows_of(k):
        return pl.ds(k * HALF, HALF)

    def onward(d):
        return 0 if d == 1 else 1

    def send_own(part, lead):
        for d in (1, -1):
            k = onward(d) if lead else 1 - onward(d)
            ref = cd.at[c, y, part, rows_of(k)]
            send(("C", part, d, k), ref, ref, ydev(d, c))

    send_own(0, True)
    send_own(0, False)
    send(("CP", 0), cd.at[c, y, 0], cd.at[c, y, 0], partner)
    for m in range(2):
        send(("PR", m), pb.at[m], g.at[m, :, c], partner)
        g[m, :, c] = gv[source(m * 8 + r)].reshape(STRIPS, STRIP, BLK)
    load_diag.wait()
    cd[c, y, 1] = dv[source(t)]
    load_front.start()
    send_own(1, True)

    def piece(m, dp, dq, part=None):
        at = strip(m, dp, dq)
        if part is None:
            return g.at[m, at, pl.ds(2, 6)]
        return g.at[m, at, pl.ds(2 + 3 * part, 3)]

    def item_ref(m, item, dq):
        if item == "own":
            return piece(m, 0, dq)
        if item in (1, -1):
            return piece(m, item, dq)
        return piece(m, 2, dq, 0 if item == 2 else 1)

    def half_ref(m, item, dq, part):
        if item == "own":
            return piece(m, 0, dq, part)
        if item in (1, -1):
            return piece(m, item, dq, part)
        return piece(m, 2, dq, part)

    def first_q(m, item):
        for d in (1, -1):
            ref = item_ref(m, item, 0)
            send(("B1", m, item, d), ref, ref, dev(m, 0, d))

    def second_q(m, item):
        for d in (1, -1):
            arrived(("B1", m, item, d), item_ref(m, item, -d))
            ref = half_ref(m, item, -d, onward(d))
            send(("B2", m, item, d), ref, ref, dev(m, 0, d))

    def second_q_far(m):
        for d in (1, -1):
            for item in (2, -2):
                arrived(("B1", m, item, d), item_ref(m, item, -d))
        for d in (1, -1):
            item = 2 * d
            ref = item_ref(m, item, -d)
            send(("B2", m, item, d), ref, ref, dev(m, 0, d))

    def relay(part):
        for d in (1, -1):
            k = onward(d)
            half = cd.at[c, wrap(y - d), part, rows_of(k)]
            arrived(("C", part, d, k), half)
            send(("CF", part, d), half, half, ydev(d, c))

    def near(part):
        for d in (1, -1):
            k = 1 - onward(d)
            arrived(("C", part, d, k), cd.at[c, wrap(y - d), part, rows_of(k)])
            ref = cd.at[c, wrap(y - d), part]
            send(("CN", part, d), ref, ref, partner)

    def far(part):
        for d in (1, -1):
            half = cd.at[c, wrap(y + 2), part, rows_of(onward(d))]
            arrived(("CF", part, d), half)
            send(("CQ", part, d), half, half, partner)

    def partner_blocks(part):
        arrived(("CP", part), cd.at[other, y, part])
        for d in (1, -1):
            arrived(("CN", part, d), cd.at[other, wrap(y - d), part])
            arrived(("CQ", part, d), cd.at[other, wrap(y + 2), part, rows_of(onward(d))])

    zero = jnp.zeros((), jnp.bfloat16)
    down = lax.broadcasted_iota(jnp.int32, (BLK, BLK), 0)

    def project(s, _):
        for child in range(2):
            count = kept(child, s, s * WINDOW + t)
            col = jnp.where(down < count, cd[child, s, 0], zero)
            proj = lax.dot_general(
                cw[child], col, (((0,), (1,)), ((), ())), preferred_element_type=jnp.float32
            )
            pt[s, child * BLK:(child + 1) * BLK, :] = proj.astype(jnp.bfloat16)
        return 0

    def add_tiles(m, groups, first, rows, unroll):
        for n, d in enumerate(groups):
            s = wrap(y + d)
            for child in range(2):
                count = kept(child, s, (2 * s + m) * 8 + r)
                block = g[m, pl.ds(first, rows // STRIP), 2 * d + child].reshape(rows, BLK)
                inside = down[:rows] + first * STRIP < count
                ascr[n * rows:(n + 1) * rows, child * BLK:(child + 1) * BLK] = jnp.where(inside, block, zero)

        def column(b):
            tile = jnp.dot(
                ascr[:len(groups) * rows, :], pt[b], preferred_element_type=jnp.float32
            )
            for n, d in enumerate(groups):
                dst = front.at[2 * wrap(y + d) + m]
                for side in range(2):
                    at = pl.ds(first * STRIP * 8 + side * CHIPS + b, rows, stride=8)
                    dst[at, :] = dst[at, :] + tile[n * rows:(n + 1) * rows, side * LANES:(side + 1) * LANES]

        @pl.loop(0, CHIPS // unroll)
        def _(i):
            for k in range(unroll):
                column(i * unroll + k)

    def quarter(m, dq):
        line = z * (1 - m) + x * m
        add_tiles(m, (1, 2, 3), SIDE * wrap(line + dq), SIDE * STRIP, 2)

    def add_diagonals():
        cols = lax.broadcasted_iota(jnp.int32, (BLK, LANES), 1)
        for b in range(CHIPS):
            dst = front.at[2 * b + t // 8]
            for side in range(2):
                at = pl.ds(side * CHIPS + b, BLK, stride=8)
                total = dst[at, :]
                for child in range(2):
                    count = kept(child, b, b * WINDOW + t)
                    inside = jnp.logical_and(down[:, :LANES] < count, cols + side * LANES < count)
                    block = cd[child, b, 1, :, side * LANES:(side + 1) * LANES].astype(jnp.float32)
                    total = total + jnp.where(inside, block, 0.0)
                dst[at, :] = total

    for m in range(2):
        for d in (1, 2, 3):
            for k in range(CORES):
                arrived(("S", m, (d - 1) * CORES + k), g.at[m, strip(m, 0, 0), 2 * d + k])
    for m in range(2):
        for d in (1, -1):
            ref = piece(m, 0, 0)
            send(("A1", m, d), ref, ref, dev(m, d, 0))
    for m in range(2):
        first_q(m, "own")
    send(("CP", 1), cd.at[c, y, 1], cd.at[c, y, 1], partner)
    relay(0)
    send_own(1, False)
    near(0)
    for m in range(2):
        for d in (1, -1):
            arrived(("A1", m, d), piece(m, -d, 0))
            ref = piece(m, -d, 0, onward(d))
            send(("A2", m, d), ref, ref, dev(m, d, 0))
        for d in (1, -1):
            first_q(m, -d)
    for m in range(2):
        second_q(m, "own")
    relay(1)
    for m in range(2):
        for d in (1, -1):
            arrived(("A2", m, d), piece(m, 2, 0, onward(d)))
            first_q(m, 2 * d)
    far(0)
    load_front.wait()
    load_coup.wait()
    for m in range(2):
        for d in (1, -1):
            second_q(m, d)
    near(1)
    partner_blocks(0)
    lax.fori_loop(0, CHIPS, project, 0)
    for m in range(2):
        second_q_far(m)
    far(1)
    for m in range(2):
        arrived(("PR", m), g.at[m, :, other])

    @pl.loop(0, 2)
    def _(m):
        add_tiles(m, (0,), 0, BLK, 1)

    @pl.loop(0, 6)
    def _(i):
        quarter(i // 3, i % 3 - 1)

    partner_blocks(1)

    @pl.when(r == t % 8)
    def _():
        add_diagonals()

    for m in range(2):
        for d in (1, -1):
            for item in ("own", 1, -1, 2 * d):
                arrived(("B2", m, item, d), half_ref(m, item, 2, onward(d)))

    @pl.loop(0, 2)
    def _(m):
        quarter(m, 2)

    for copy in sent:
        copy.wait_send()


def write_kernel(front, out, sems):
    copies = [pltpu.make_async_copy(front.at[a], out.at[a], sems.at[a]) for a in range(8)]
    for copy in copies:
        copy.start()
    for copy in copies:
        copy.wait()


def shards(parent_front, generators, diagonal_blocks, coupling, block_map, valid_rows):
    flat = parent_front.reshape(8, BLK, CHIPS, 2, LANES).transpose(0, 1, 3, 2, 4).reshape(8, BLK * 8, LANES)
    any_spec = pl.BlockSpec(memory_space=pl.ANY)
    vmem = pl.BlockSpec(memory_space=pltpu.VMEM)
    smem = pl.BlockSpec(memory_space=pltpu.SMEM)
    bf16 = jnp.bfloat16
    front = pl.pallas_call(
        gather_kernel,
        name="gather",
        in_specs=[smem, smem, any_spec, any_spec, any_spec, any_spec],
        out_specs=vmem,
        out_shape=pltpu.VMEM((8, BLK * 8, LANES), jnp.float32),
        scratch_shapes=[
            pltpu.VMEM((2, STRIPS, UNITS, STRIP, BLK), bf16),
            pltpu.VMEM((2, CHIPS, 2, BLK, BLK), bf16),
            pltpu.VMEM((2, GROUP, STRIP, BLK), bf16),
            pltpu.VMEM((GROUP, BLK, BLK), bf16),
            pltpu.VMEM((GROUP, BLK, BLK), bf16),
            pltpu.VMEM((2, BLK, BLK), bf16),
            pltpu.VMEM((2, 6, STRIP, BLK), bf16),
            pltpu.VMEM((2, STRIPS, STRIP, BLK), bf16),
            pltpu.VMEM((CHIPS, 2 * BLK, BLK), bf16),
            pltpu.VMEM((BLK, 2 * BLK), bf16),
            pltpu.SemaphoreType.DMA((6,)),
            pltpu.SemaphoreType.DMA((len(SEMS),)),
            pltpu.SemaphoreType.DMA((len(SEMS),)),
        ],
        compiler_params=pltpu.CompilerParams(
            collective_id=0, has_side_effects=True, vmem_limit_bytes=52 << 20
        ),
    )(block_map, valid_rows, generators, diagonal_blocks, coupling, flat)
    out = pl.pallas_call(
        write_kernel,
        name="write",
        in_specs=[vmem],
        out_specs=any_spec,
        out_shape=jax.ShapeDtypeStruct((8, BLK * 8, LANES), jnp.float32),
        scratch_shapes=[pltpu.SemaphoreType.DMA((8,))],
        compiler_params=pltpu.CompilerParams(vmem_limit_bytes=1 << 20),
    )(front)
    return out.reshape(8, BLK, 2, CHIPS, LANES).transpose(0, 1, 3, 2, 4).reshape(8, BLK, CHIPS, BLK)


def solution(mesh):
    in_specs = (
        P(None, "row", None, "col"),
        P("row", None, None),
        P("row", None, None),
        P(),
        P(),
        P(),
    )
    out_specs = P(None, "row", None, "col")
    return jax.shard_map(shards, mesh=mesh, in_specs=in_specs, out_specs=out_specs, check_vma=False)
```

time: 95 us -> 39.3 us (0.41)
  Pallas kernels: 0 us -> 39.2 us
  waiting for transfers between devices: 35.5 us -> 0 us
  local copies, waits for them, and re-layouts: 18.4 us -> 0 us
  between operations: 13.5 us -> 0.01 us
  other arithmetic: 12.2 us -> 0 us
  matrix products: 10.1 us -> 0 us
  starting transfers between devices: 4.58 us -> 0 us
    pallas_call x0 -> x2, Pallas kernels: none -> 39.2 us  [the longest x1 35.8 us: shards(): pl.pallas_call(gather_kernel, name='gather', in_specs=[smem, smem, any_sp...]
    all_to_all x1 -> x0, waiting for transfers between devices: 35.5 us -> none  [shards(): lax.all_to_all(row_send, 'row', split_axis=0, concat_axis=0, tiled=True)]
    add x1 -> x0, local copies, waits for them, and re-layouts: 12.2 us -> none  [shards(): running = running + rounded.astype(jnp.float32)]
    add x3 -> x0, other arithmetic: 10.5 us -> none  [the longest x1 10.5 us: shards(): running = running + rounded.astype(jnp.float32)]
    dot_general x6 -> x0, matrix products: 10.1 us -> none  [the longest x2 4.84 us: shards(): jnp.einsum('axq,bzq->axbz', row_received[child_index], col_received[child...]
    all_to_all x1 -> x0, starting transfers between devices: 4.58 us -> none  [shards(): lax.all_to_all(row_send, 'row', split_axis=0, concat_axis=0, tiled=True)]
    convert_element_type x2 -> x0, local copies, waits for them, and re-layouts: 2.98 us -> none  [the longest x1 2.94 us: shards(): row_send = jnp.einsum('kri,ixq->rkxq', row_place, masked, preferred_eleme...]
    slice x2 -> x0, local copies, waits for them, and re-layouts: 1.82 us -> none  [the longest x1 1.68 us: sent_together(): outs.append(lax.slice_in_dim(filled, at, at + a.shape[along], axis=along))]
  transfers between devices with their start and end apart: 2 -> 0, of which waited for: 1 -> 0; matrix products, arithmetic and copies ran while one was open for 5% -> 0% of each run, Pallas kernels for 0% -> 0%
where the time goes in v2:
time: 39.3 us; the launch traced here: 39.2 us
  Pallas kernels  39.2 us (100%)
    pallas_call x1, Pallas kernels, shards(): pl.pallas_call(gather_kernel, name='gather', in_specs=[smem, smem, any_sp...  35.8 us
    pallas_call x1, Pallas kernels, shards(): pl.pallas_call(write_kernel, name='write', in_specs=[vmem], out_specs=any...  3.37 us

profile of v2, /device:TPU:0, one launch (start us, length us, event | category | flops | bytes accessed | tf_op | source)
XLA Modules:
  0.0 39.2 jit_solution(16364787653226088422)
XLA Ops:
  0.0 35.8 %gather.1.front = f32[8,2048,128]{2,1,0:T(8,128)S(1)} custom-call(s32[2,48]{1,0:T(2,128)} %bmap.1, s32[2,48]{1,0:T(2,128)} %vrows.1, bf16[12,256,256]{2,1,0:T(8,128)(2,1)} %gen.1, bf16[12,256,256]{2,1,0:T(8,128)(2,1)} %diag.1, bf16[2,256,256]{2,1,0:T(8,128)(2,1)} %coup.1, f32[8,2048,128]{2,1,0:T(8,128)} %bitcast.10), custom_call_target="tpu_custom_call" | custom-call | tf_op jit(solution)/shard_map/gather/pallas_call | solution.py:371
  35.8 3.4 %write.1 = f32[8,2048,128]{2,1,0:T(8,128)} custom-call(f32[8,2048,128]{2,1,0:T(8,128)S(1)} %gather.1.front), custom_call_target="tpu_custom_call" | custom-call | tf_op jit(solution)/shard_map/write/pallas_call | solution.py:396

commit v3 on v2

--- a/solution.py
+++ b/solution.py
@@ -14,9 +14,9 @@
 STRIPS = 16
 BLK = 256
 STRIP = BLK // STRIPS
-UNITS = 2 * CHIPS
 LANES = 128
 HALF = BLK // 2
+BANDS = 8
 
 
 def semaphore_table():
@@ -41,7 +41,7 @@
 
 
 def gather_kernel(
-    bmap, vrows, gen, diag, coup, parent, front, g, cd, gp, gv, dv, cw, sb, pb, pt, ascr, lsem, ssem, rsem
+    bmap, vrows, gen, diag, coup, parent, front, g, cd, gp, gv, dv, cw, sb, pb, pt, lsem, fsem, ssem, rsem
 ):
     r = lax.axis_index("row")
     t = lax.axis_index("col")
@@ -64,14 +64,18 @@
     def strip(m, dp, dq):
         return wrap(pos[m][1] + dq) * SIDE + wrap(pos[m][0] + dp)
 
+    own_strip = [strip(0, 0, 0), strip(1, 0, 0)]
     load_strips = [
-        pltpu.make_async_copy(gen.at[:, pl.ds(strip(m, 0, 0) * STRIP, STRIP), :], gp.at[m], lsem.at[m])
+        pltpu.make_async_copy(gen.at[:, pl.ds(own_strip[m] * STRIP, STRIP), :], gp.at[m], lsem.at[m])
         for m in range(2)
     ]
     load_gen = pltpu.make_async_copy(gen, gv, lsem.at[2])
     load_diag = pltpu.make_async_copy(diag, dv, lsem.at[3])
     load_coup = pltpu.make_async_copy(coup, cw, lsem.at[4])
-    load_front = pltpu.make_async_copy(parent, front, lsem.at[5])
+    load_front = [
+        pltpu.make_async_copy(parent.at[a, :, band, 0, :], front.at[a, band], fsem.at[a * BANDS + band])
+        for a in range(8) for band in range(BANDS)
+    ]
     for load in load_strips:
         load.start()
 
@@ -91,21 +95,21 @@
         before = jnp.int32(0)
         for e in entries:
             before = before + jnp.where(e < at, 1, 0).astype(jnp.int32)
-        return jnp.minimum(before, GROUP - 1)
-
-    def kept(child, group, parent_block):
-        total = jnp.int32(0)
-        for i in range(GROUP):
-            at = group * GROUP + i
-            total = total + jnp.where(bmap[child, at] == parent_block, vrows[child, at], 0)
-        return total
+        index = jnp.minimum(before, GROUP - 1)
+        there = bmap[c, y * GROUP + index] == at
+        return index, jnp.where(there, vrows[c, y * GROUP + index], 0)
+
+    zero = jnp.zeros((), jnp.bfloat16)
+    down = lax.broadcasted_iota(jnp.int32, (BLK, BLK), 0)
 
     for load in load_strips:
         load.wait()
     for m in range(2):
         for d in (2, 1, 3):
             for k in range(CORES):
-                sb[m, (d - 1) * CORES + k] = gp[m, source(m * 8 + CORES * wrap(y - d) + k)]
+                index, count = source(m * 8 + CORES * wrap(y - d) + k)
+                inside = down[:STRIP] + own_strip[m] * STRIP < count
+                sb[m, (d - 1) * CORES + k] = jnp.where(inside, gp[m, index], zero)
 
     pl.semaphore_wait(barrier, len(peers))
 
@@ -132,13 +136,15 @@
             for k in range(CORES):
                 i = (d - 1) * CORES + k
                 send(
-                    ("S", m, i), sb.at[m, i], g.at[m, strip(m, 0, 0), 2 * d + c],
+                    ("S", m, i), sb.at[m, i], g.at[m, own_strip[m], d, c],
                     ydev(-d, k), SEMS[("S", m, 0)] + (d - 1) * CORES + c,
                 )
     load_gen.wait()
-    cd[c, y, 0] = gv[source(t)]
-    for m in range(2):
-        pb[m] = gv[source(m * 8 + y * CORES + other)].reshape(STRIPS, STRIP, BLK)
+    index, wanted = source(t)
+    cd[c, y, 0] = jnp.where(down < wanted, gv[index], zero)
+    for m in range(2):
+        index, count = source(m * 8 + y * CORES + other)
+        pb[m] = jnp.where(down < count, gv[index], zero).reshape(STRIPS, STRIP, BLK)
 
     def rows_of(k):
         return pl.ds(k * HALF, HALF)
@@ -156,18 +162,25 @@
     send_own(0, False)
     send(("CP", 0), cd.at[c, y, 0], cd.at[c, y, 0], partner)
     for m in range(2):
-        send(("PR", m), pb.at[m], g.at[m, :, c], partner)
-        g[m, :, c] = gv[source(m * 8 + r)].reshape(STRIPS, STRIP, BLK)
+        send(("PR", m), pb.at[m], g.at[m, :, 0, c], partner)
+        index, count = source(m * 8 + r)
+        g[m, :, 0, c] = jnp.where(down < count, gv[index], zero).reshape(STRIPS, STRIP, BLK)
     load_diag.wait()
-    cd[c, y, 1] = dv[source(t)]
-    load_front.start()
+    across = lax.broadcasted_iota(jnp.int32, (BLK, BLK), 1)
+    index, count = source(t)
+    cd[c, y, 1] = jnp.where(jnp.logical_and(down < count, across < count), dv[index], zero)
+    for load in load_front:
+        load.start()
     send_own(1, True)
+    load_coup.wait()
+    for child in range(2):
+        cw[child] = cw[child].T
 
     def piece(m, dp, dq, part=None):
         at = strip(m, dp, dq)
         if part is None:
-            return g.at[m, at, pl.ds(2, 6)]
-        return g.at[m, at, pl.ds(2 + 3 * part, 3)]
+            return g.at[m, at, pl.ds(1, 3)]
+        return g.at[m, at, pl.ds(1, 3), part]
 
     def item_ref(m, item, dq):
         if item == "own":
@@ -223,71 +236,62 @@
             arrived(("CF", part, d), half)
             send(("CQ", part, d), half, half, partner)
 
-    def partner_blocks(part):
+    def partner_own(part):
         arrived(("CP", part), cd.at[other, y, part])
+
+    def partner_near(part):
         for d in (1, -1):
             arrived(("CN", part, d), cd.at[other, wrap(y - d), part])
+
+    def partner_far(part):
+        for d in (1, -1):
             arrived(("CQ", part, d), cd.at[other, wrap(y + 2), part, rows_of(onward(d))])
 
-    zero = jnp.zeros((), jnp.bfloat16)
-    down = lax.broadcasted_iota(jnp.int32, (BLK, BLK), 0)
-
-    def project(s, _):
+    def project(s):
         for child in range(2):
-            count = kept(child, s, s * WINDOW + t)
-            col = jnp.where(down < count, cd[child, s, 0], zero)
             proj = lax.dot_general(
-                cw[child], col, (((0,), (1,)), ((), ())), preferred_element_type=jnp.float32
+                cw[child], cd[child, s, 0], (((1,), (1,)), ((), ())), preferred_element_type=jnp.float32
             )
-            pt[s, child * BLK:(child + 1) * BLK, :] = proj.astype(jnp.bfloat16)
-        return 0
-
-    def add_tiles(m, groups, first, rows, unroll):
-        for n, d in enumerate(groups):
-            s = wrap(y + d)
-            for child in range(2):
-                count = kept(child, s, (2 * s + m) * 8 + r)
-                block = g[m, pl.ds(first, rows // STRIP), 2 * d + child].reshape(rows, BLK)
-                inside = down[:rows] + first * STRIP < count
-                ascr[n * rows:(n + 1) * rows, child * BLK:(child + 1) * BLK] = jnp.where(inside, block, zero)
-
-        def column(b):
-            tile = jnp.dot(
-                ascr[:len(groups) * rows, :], pt[b], preferred_element_type=jnp.float32
-            )
-            for n, d in enumerate(groups):
-                dst = front.at[2 * wrap(y + d) + m]
-                for side in range(2):
-                    at = pl.ds(first * STRIP * 8 + side * CHIPS + b, rows, stride=8)
-                    dst[at, :] = dst[at, :] + tile[n * rows:(n + 1) * rows, side * LANES:(side + 1) * LANES]
-
-        @pl.loop(0, CHIPS // unroll)
-        def _(i):
-            for k in range(unroll):
-                column(i * unroll + k)
+            pt[s, child] = proj.astype(jnp.bfloat16)
+
+    def multiply(left, b):
+        tile = jnp.dot(left[0], pt[b, 0], preferred_element_type=jnp.float32)
+        return tile + jnp.dot(left[1], pt[b, 1], preferred_element_type=jnp.float32)
+
+    def add_to(a, first, rows, b, tile):
+        at = pl.ds(first, rows)
+        for side in range(2):
+            band = side * CHIPS + b
+            front[a, band, at] = front[a, band, at] + tile[:, side * LANES:(side + 1) * LANES]
+
+    def own_tiles(b):
+        for m in range(2):
+            left = [g[m, :, 0, child].reshape(BLK, BLK) for child in range(2)]
+            add_to(2 * y + m, 0, BLK, b, multiply(left, b))
 
     def quarter(m, dq):
         line = z * (1 - m) + x * m
-        add_tiles(m, (1, 2, 3), SIDE * wrap(line + dq), SIDE * STRIP, 2)
+        first = SIDE * wrap(line + dq)
+        left = [g[m, pl.ds(first, SIDE), 1:CHIPS, child].reshape(3 * SIDE * STRIP, BLK) for child in range(2)]
+        for b in range(CHIPS):
+            tile = multiply(left, b)
+            for n in range(SIDE):
+                for d in (1, 2, 3):
+                    at = (n * 3 + d - 1) * STRIP
+                    add_to(2 * wrap(y + d) + m, (first + n) * STRIP, STRIP, b, tile[at:at + STRIP])
 
     def add_diagonals():
-        cols = lax.broadcasted_iota(jnp.int32, (BLK, LANES), 1)
         for b in range(CHIPS):
-            dst = front.at[2 * b + t // 8]
-            for side in range(2):
-                at = pl.ds(side * CHIPS + b, BLK, stride=8)
-                total = dst[at, :]
-                for child in range(2):
-                    count = kept(child, b, b * WINDOW + t)
-                    inside = jnp.logical_and(down[:, :LANES] < count, cols + side * LANES < count)
-                    block = cd[child, b, 1, :, side * LANES:(side + 1) * LANES].astype(jnp.float32)
-                    total = total + jnp.where(inside, block, 0.0)
-                dst[at, :] = total
-
-    for m in range(2):
-        for d in (1, 2, 3):
+            total = cd[0, b, 1].astype(jnp.float32) + cd[1, b, 1].astype(jnp.float32)
+            add_to(2 * b + t // 8, 0, BLK, b, total)
+
+    for d in (1, 3):
+        for m in range(2):
             for k in range(CORES):
-                arrived(("S", m, (d - 1) * CORES + k), g.at[m, strip(m, 0, 0), 2 * d + k])
+                arrived(("S", m, (d - 1) * CORES + k), g.at[m, own_strip[m], d, k])
+    for m in range(2):
+        for k in range(CORES):
+            arrived(("S", m, CORES + k), g.at[m, own_strip[m], 2, k])
     for m in range(2):
         for d in (1, -1):
             ref = piece(m, 0, 0)
@@ -308,34 +312,45 @@
     for m in range(2):
         second_q(m, "own")
     relay(1)
+    partner_own(0)
+    partner_near(0)
+    for load in load_front:
+        load.wait()
+    for m in range(2):
+        arrived(("PR", m), g.at[m, :, 0, other])
+
+    @pl.loop(0, 3)
+    def _(i):
+        project(wrap(y + i - 1))
+
     for m in range(2):
         for d in (1, -1):
             arrived(("A2", m, d), piece(m, 2, 0, onward(d)))
             first_q(m, 2 * d)
     far(0)
-    load_front.wait()
-    load_coup.wait()
+
+    @pl.loop(0, 3)
+    def _(i):
+        own_tiles(wrap(y + i - 1))
+
     for m in range(2):
         for d in (1, -1):
             second_q(m, d)
     near(1)
-    partner_blocks(0)
-    lax.fori_loop(0, CHIPS, project, 0)
+    partner_far(0)
+    project(wrap(y + 2))
+    own_tiles(wrap(y + 2))
     for m in range(2):
         second_q_far(m)
     far(1)
-    for m in range(2):
-        arrived(("PR", m), g.at[m, :, other])
-
-    @pl.loop(0, 2)
-    def _(m):
-        add_tiles(m, (0,), 0, BLK, 1)
 
     @pl.loop(0, 6)
     def _(i):
         quarter(i // 3, i % 3 - 1)
 
-    partner_blocks(1)
+    partner_own(1)
+    partner_near(1)
+    partner_far(1)
 
     @pl.when(r == t % 8)
     def _():
@@ -355,7 +370,10 @@
 
 
 def write_kernel(front, out, sems):
-    copies = [pltpu.make_async_copy(front.at[a], out.at[a], sems.at[a]) for a in range(8)]
+    copies = [
+        pltpu.make_async_copy(front.at[a, band], out.at[a, :, band, 0, :], sems.at[a * BANDS + band])
+        for a in range(8) for band in range(BANDS)
+    ]
     for copy in copies:
         copy.start()
     for copy in copies:
@@ -363,7 +381,7 @@
 
 
 def shards(parent_front, generators, diagonal_blocks, coupling, block_map, valid_rows):
-    flat = parent_front.reshape(8, BLK, CHIPS, 2, LANES).transpose(0, 1, 3, 2, 4).reshape(8, BLK * 8, LANES)
+    banded = parent_front.reshape(8, BLK, CHIPS, 2, LANES).transpose(0, 1, 3, 2, 4).reshape(8, BLK, BANDS, 1, LANES)
     any_spec = pl.BlockSpec(memory_space=pl.ANY)
     vmem = pl.BlockSpec(memory_space=pltpu.VMEM)
     smem = pl.BlockSpec(memory_space=pltpu.SMEM)
@@ -373,9 +391,9 @@
         name="gather",
         in_specs=[smem, smem, any_spec, any_spec, any_spec, any_spec],
         out_specs=vmem,
-        out_shape=pltpu.VMEM((8, BLK * 8, LANES), jnp.float32),
+        out_shape=pltpu.VMEM((8, BANDS, BLK, LANES), jnp.float32),
         scratch_shapes=[
-            pltpu.VMEM((2, STRIPS, UNITS, STRIP, BLK), bf16),
+            pltpu.VMEM((2, STRIPS, CHIPS, 2, STRIP, BLK), bf16),
             pltpu.VMEM((2, CHIPS, 2, BLK, BLK), bf16),
             pltpu.VMEM((2, GROUP, STRIP, BLK), bf16),
             pltpu.VMEM((GROUP, BLK, BLK), bf16),
@@ -383,23 +401,23 @@
             pltpu.VMEM((2, BLK, BLK), bf16),
             pltpu.VMEM((2, 6, STRIP, BLK), bf16),
             pltpu.VMEM((2, STRIPS, STRIP, BLK), bf16),
-            pltpu.VMEM((CHIPS, 2 * BLK, BLK), bf16),
-            pltpu.VMEM((BLK, 2 * BLK), bf16),
-            pltpu.SemaphoreType.DMA((6,)),
+            pltpu.VMEM((CHIPS, 2, BLK, BLK), bf16),
+            pltpu.SemaphoreType.DMA((5,)),
+            pltpu.SemaphoreType.DMA((8 * BANDS,)),
             pltpu.SemaphoreType.DMA((len(SEMS),)),
             pltpu.SemaphoreType.DMA((len(SEMS),)),
         ],
         compiler_params=pltpu.CompilerParams(
             collective_id=0, has_side_effects=True, vmem_limit_bytes=52 << 20
         ),
-    )(block_map, valid_rows, generators, diagonal_blocks, coupling, flat)
+    )(block_map, valid_rows, generators, diagonal_blocks, coupling, banded)
     out = pl.pallas_call(
         write_kernel,
         name="write",
         in_specs=[vmem],
         out_specs=any_spec,
-        out_shape=jax.ShapeDtypeStruct((8, BLK * 8, LANES), jnp.float32),
-        scratch_shapes=[pltpu.SemaphoreType.DMA((8,))],
+        out_shape=jax.ShapeDtypeStruct((8, BLK, BANDS, 1, LANES), jnp.float32),
+        scratch_shapes=[pltpu.SemaphoreType.DMA((8 * BANDS,))],
         compiler_params=pltpu.CompilerParams(vmem_limit_bytes=1 << 20),
     )(front)
     return out.reshape(8, BLK, 2, CHIPS, LANES).transpose(0, 1, 3, 2, 4).reshape(8, BLK, CHIPS, BLK)

time: 39.3 us -> 34.4 us (0.88)
  Pallas kernels: 39.2 us -> 34.3 us
    pallas_call x1, Pallas kernels: 35.8 us -> 30.5 us  [shards(): pl.pallas_call(gather_kernel, name='gather', in_specs=[smem, smem, any_sp...]
    pallas_call x1, Pallas kernels: 3.37 us -> 3.8 us  [shards(): pl.pallas_call(write_kernel, name='write', in_specs=[vmem], out_specs=any...]
where the time goes in v3:
time: 34.4 us; the launch traced here: 34.3 us
  Pallas kernels  34.3 us (100%)
    pallas_call x1, Pallas kernels, shards(): pl.pallas_call(gather_kernel, name='gather', in_specs=[smem, smem, any_sp...  30.5 us
    pallas_call x1, Pallas kernels, shards(): pl.pallas_call(write_kernel, name='write', in_specs=[vmem], out_specs=any...  3.8 us

profile of v3, /device:TPU:0, one launch (start us, length us, event | category | flops | bytes accessed | tf_op | source)
XLA Modules:
  0.0 34.3 jit_solution(4869040409166904741)
XLA Ops:
  0.0 30.5 %gather.1.front = f32[8,8,256,128]{3,2,1,0:T(8,128)S(1)} custom-call(s32[2,48]{1,0:T(2,128)} %bmap.1, s32[2,48]{1,0:T(2,128)} %vrows.1, bf16[12,256,256]{2,1,0:T(8,128)(2,1)} %gen.1, bf16[12,256,256]{2,1,0:T(8,128)(2,1)} %diag.1, bf16[2,256,256]{2,1,0:T(8,128)(2,1)} %coup.1, f32[8,256,8,1,128]{4,3,2,1,0:T(1,128)} %bitcast.10), custom_call_target="tpu_custom_call" | custom-call | tf_op jit(solution)/shard_map/gather/pallas_call | solution.py:389
  30.5 3.8 %write.1 = f32[8,256,8,1,128]{4,3,2,1,0:T(1,128)} custom-call(f32[8,8,256,128]{3,2,1,0:T(8,128)S(1)} %gather.1.front), custom_call_target="tpu_custom_call" | custom-call | tf_op jit(solution)/shard_map/write/pallas_call | solution.py:414

commit v4 on v3

v4 whole, which is shorter than its diff:
```python
import math

import jax
import jax.numpy as jnp
from jax import lax
from jax.experimental import pallas as pl
from jax.experimental.pallas import tpu as pltpu
from jax.sharding import PartitionSpec as P

MESH = pl.DeviceIdType.MESH
CHIPS = 4
CORES = 2
SIDE = 4
GROUP = 12
WINDOW = 16
STRIPS = 16
BLK = 256
STRIP = BLK // STRIPS
LANES = 128
HALF = BLK // 2
BANDS = 8


def arrival_groups():
    names = ["S", "PR", "P0", "N0", "Q0", "P1"]
    for m in range(2):
        names += [("A1", m), ("A2", m), ("B1", m, 0), ("B1", m, 1), ("B1", m, 2), ("B2", m)]
    for part in range(2):
        names += [("CL", part), ("CO", part), ("CF", part)]
    return {name: i for i, name in enumerate(names)}


GROUPS = arrival_groups()


def product(left, pt, b):
    tile = jnp.dot(left[0], pt[b, 0], preferred_element_type=jnp.float32)
    return tile + jnp.dot(left[1], pt[b, 1], preferred_element_type=jnp.float32)


def add_block(front, a, first, rows, b, tile):
    at = pl.ds(first, rows)
    for side in range(2):
        band = side * CHIPS + b
        front[a, band, at] = front[a, band, at] + tile[:, side * LANES:(side + 1) * LANES]


def quarter_rows(g, m, first):
    return [g[m, pl.ds(first, SIDE), 1:CHIPS, child].reshape(3 * SIDE * STRIP, BLK) for child in range(2)]


def add_quarter(front, y, m, first, b, tile):
    for n in range(SIDE):
        for d in (1, 2, 3):
            at = (n * 3 + d - 1) * STRIP
            add_block(front, 2 * ((y + d) % CHIPS) + m, (first + n) * STRIP, STRIP, b, tile[at:at + STRIP])


def gather_kernel(
    maps, counts, gen, diag, coup, parent, front, g, pt, bmap, vrows, cd, gp, gv, dv, cw, sb, pb, lsem, ssem, rsem
):
    r = lax.axis_index("row")
    t = lax.axis_index("col")
    y, c = r // CORES, r % CORES
    z, x = t // SIDE, t % SIDE
    other = 1 - c
    partner = (y * CORES + other, t)
    pos = [(x, z), (z, x)]

    def wrap(v):
        return (v + 8) % 4

    def ydev(step, core):
        return (wrap(y + step) * CORES + core, t)

    def dev(m, dp, dq):
        p, q = wrap(pos[m][0] + dp), wrap(pos[m][1] + dq)
        return (r, q * SIDE + p) if m == 0 else (r, p * SIDE + q)

    def strip(m, dp, dq):
        return wrap(pos[m][1] + dq) * SIDE + wrap(pos[m][0] + dp)

    barrier = pltpu.get_barrier_semaphore()
    peers = [ydev(s, k) for s in (2, 1, 3) for k in range(CORES)] + [partner]
    peers += [dev(m, s, 0) for s in (2, 1, -1) for m in range(2)]
    for peer in peers:
        pl.semaphore_signal(barrier, inc=1, device_id=peer, device_id_type=MESH)

    own_strip = [strip(0, 0, 0), strip(1, 0, 0)]
    load_strips = [
        pltpu.make_async_copy(gen.at[:, pl.ds(own_strip[m] * STRIP, STRIP), :], gp.at[m], lsem.at[0])
        for m in range(2)
    ]
    load_tables = [pltpu.make_async_copy(maps, bmap, lsem.at[1]), pltpu.make_async_copy(counts, vrows, lsem.at[2])]
    load_gen = pltpu.make_async_copy(gen, gv, lsem.at[3])
    load_diag = pltpu.make_async_copy(diag, dv, lsem.at[4])
    load_coup = pltpu.make_async_copy(coup, cw, lsem.at[5])
    load_front = [
        pltpu.make_async_copy(parent.at[a, :, band, 0, :], front.at[a, band], lsem.at[6])
        for a in range(8) for band in range(BANDS)
    ]
    for load in load_strips + load_tables + [load_gen, load_diag, load_coup]:
        load.start()
    zero = jnp.zeros((), jnp.bfloat16)
    down = lax.broadcasted_iota(jnp.int32, (BLK, BLK), 0)
    pltpu.make_async_copy(gp, gp, lsem.at[0]).wait()
    for load in load_tables:
        load.wait()

    entries = [bmap[c, y * GROUP + i] for i in range(GROUP)]

    def source(slot):
        at = y * WINDOW + slot
        before = jnp.int32(0)
        for e in entries:
            before = before + jnp.where(e < at, 1, 0).astype(jnp.int32)
        index = jnp.minimum(before, GROUP - 1)
        there = bmap[c, y * GROUP + index] == at
        return index, jnp.where(there, vrows[c, y * GROUP + index], 0)

    for m in range(2):
        for d in (2, 1, 3):
            for k in range(CORES):
                index, count = source(m * 8 + CORES * wrap(y - d) + k)
                inside = down[:STRIP] + own_strip[m] * STRIP < count
                sb[m, (d - 1) * CORES + k] = jnp.where(inside, gp[m, index], zero)

    pl.semaphore_wait(barrier, len(peers))

    sent = []

    def send(group, src, dst, to):
        copy = pltpu.make_async_remote_copy(
            src_ref=src, dst_ref=dst, send_sem=ssem, recv_sem=rsem.at[GROUPS[group]],
            device_id=to, device_id_type=MESH,
        )
        copy.start()
        sent.append(math.prod(src.shape))

    def arrived(group, size):
        pltpu.make_async_remote_copy(
            src_ref=size, dst_ref=size, send_sem=ssem, recv_sem=rsem.at[GROUPS[group]],
            device_id=partner, device_id_type=MESH,
        ).wait_recv()

    for d in (2, 1, 3):
        for m in range(2):
            for k in range(CORES):
                i = (d - 1) * CORES + k
                send("S", sb.at[m, i], g.at[m, own_strip[m], d, c], ydev(-d, k))
    load_gen.wait()
    index, wanted = source(t)
    cd[c, y, 0] = jnp.where(down < wanted, gv[index], zero)
    for m in range(2):
        index, count = source(m * 8 + y * CORES + other)
        pb[m] = jnp.where(down < count, gv[index], zero).reshape(STRIPS, STRIP, BLK)

    def rows_of(k):
        return pl.ds(k * HALF, HALF)

    def onward(d):
        return 0 if d == 1 else 1

    def send_own(part, lead):
        for d in (1, -1):
            k = onward(d) if lead else 1 - onward(d)
            ref = cd.at[c, y, part, rows_of(k)]
            send(("CL" if lead else "CO", part), ref, ref, ydev(d, c))

    send_own(0, True)
    send_own(0, False)
    send("P0", cd.at[c, y, 0], cd.at[c, y, 0], partner)
    for m in range(2):
        send("PR", pb.at[m], g.at[m, :, 0, c], partner)
        index, count = source(m * 8 + r)
        g[m, :, 0, c] = jnp.where(down < count, gv[index], zero).reshape(STRIPS, STRIP, BLK)
    load_diag.wait()
    across = lax.broadcasted_iota(jnp.int32, (BLK, BLK), 1)
    index, count = source(t)
    cd[c, y, 1] = jnp.where(jnp.logical_and(down < count, across < count), dv[index], zero)
    for load in load_front:
        load.start()
    send_own(1, True)
    load_coup.wait()
    for child in range(2):
        cw[child] = cw[child].T

    def piece(m, dp, dq, part=None):
        at = strip(m, dp, dq)
        if part is None:
            return g.at[m, at, pl.ds(1, 3)]
        return g.at[m, at, pl.ds(1, 3), part]

    def first_q(m, item):
        for d in (1, -1):
            ref = piece(m, item, 0)
            send(("B1", m, abs(item)), ref, ref, dev(m, 0, d))

    def second_q(m, items):
        arrived(("B1", m, abs(items[0])), g.at[m, pl.ds(0, 2 * len(items)), pl.ds(1, 3)])
        for item in items:
            for d in (1, -1):
                ref = piece(m, item, -d, onward(d))
                send(("B2", m), ref, ref, dev(m, 0, d))

    one_block = cd.at[0, 0, 0]

    def relay(part):
        arrived(("CL", part), one_block)
        for d in (1, -1):
            half = cd.at[c, wrap(y - d), part, rows_of(onward(d))]
            send(("CF", part), half, half, ydev(d, c))

    def near(part):
        arrived(("CO", part), one_block)
        for d in (1, -1):
            ref = cd.at[c, wrap(y - d), part]
            send(("N0", "P1")[part], ref, ref, partner)

    def far(part):
        arrived(("CF", part), one_block)
        for d in (1, -1):
            half = cd.at[c, wrap(y + 2), part, rows_of(onward(d))]
            send(("Q0", "P1")[part], half, half, partner)

    def project(s):
        for child in range(2):
            proj = lax.dot_general(
                cw[child], cd[child, s, 0], (((1,), (1,)), ((), ())), preferred_element_type=jnp.float32
            )
            pt[s, child] = proj.astype(jnp.bfloat16)

    def add_to(a, first, rows, b, tile):
        add_block(front, a, first, rows, b, tile)

    def multiply(left, b):
        return product(left, pt, b)

    def own_tiles(b):
        for m in range(2):
            left = [g[m, :, 0, child].reshape(BLK, BLK) for child in range(2)]
            add_to(2 * y + m, 0, BLK, b, multiply(left, b))

    def quarter(m, dq):
        first = SIDE * wrap(z * (1 - m) + x * m + dq)
        left = quarter_rows(g, m, first)
        for b in range(CHIPS):
            add_quarter(front, y, m, first, b, multiply(left, b))

    def add_diagonals():
        for b in range(CHIPS):
            total = cd[0, b, 1].astype(jnp.float32) + cd[1, b, 1].astype(jnp.float32)
            add_to(2 * b + t // 8, 0, BLK, b, total)

    arrived("P0", one_block)
    project(y)
    arrived("PR", g.at[:, :, 0, 0])
    arrived("S", g.at[0, pl.ds(0, 2), pl.ds(1, 3)])
    for m in range(2):
        ref = piece(m, 0, 0)
        for d in (1, -1):
            send(("A1", m), ref, ref, dev(m, d, 0))
        send(("A2", m), ref, ref, dev(m, 2, 0))
    for m in range(2):
        first_q(m, 0)
    send("P1", cd.at[c, y, 1], cd.at[c, y, 1], partner)
    relay(0)
    send_own(1, False)
    pltpu.make_async_copy(front, front, lsem.at[6]).wait()
    own_tiles(y)
    near(0)
    for m in range(2):
        arrived(("A1", m), g.at[m, pl.ds(0, 2), pl.ds(1, 3)])
        for d in (1, -1):
            first_q(m, -d)
    for m in range(2):
        second_q(m, (0,))
    far(0)
    for m in range(2):
        arrived(("A2", m), g.at[m, 0, pl.ds(1, 3)])
        first_q(m, 2)
    relay(1)
    near(1)
    arrived("N0", cd.at[0, pl.ds(0, 2), 0])

    @pl.loop(0, 2)
    def _(i):
        project(wrap(y + 2 * i - 1))

    for m in range(2):
        second_q(m, (1, -1))

    @pl.loop(0, 2)
    def _(i):
        own_tiles(wrap(y + 2 * i - 1))

    for m in range(2):
        second_q(m, (2,))
    arrived("Q0", one_block)
    project(wrap(y + 2))
    own_tiles(wrap(y + 2))

    @pl.loop(0, 2)
    def _(m):
        quarter(m, 0)

    far(1)

    @pl.loop(0, 4)
    def _(i):
        quarter(i // 2, 2 * (i % 2) - 1)

    arrived("P1", cd.at[0, :, 1])

    @pl.when(r == t % 8)
    def _():
        add_diagonals()

    for m in range(2):
        arrived(("B2", m), g.at[m, pl.ds(0, 4), pl.ds(1, 3)])
    blocks, rest = divmod(sum(sent), 2 * CHIPS * BLK * LANES)
    assert rest == 0
    everything = front.at[pl.ds(0, blocks), pl.ds(0, CHIPS)]
    pltpu.make_async_remote_copy(
        src_ref=everything, dst_ref=everything, send_sem=ssem, recv_sem=rsem.at[0],
        device_id=partner, device_id_type=MESH,
    ).wait_send()


def write_kernel(taken, g, pt, out, front, done):
    y = lax.axis_index("row") // CORES
    t = lax.axis_index("col")
    lines = [t // SIDE, t % SIDE]

    def write(a, b):
        for side in range(2):
            band = side * CHIPS + b
            pltpu.make_async_copy(front.at[a, band], out.at[a, :, band, 0, :], done).start()

    for m in range(2):
        for b in range(CHIPS):
            write(2 * y + m, b)
    for m in range(2):
        first = SIDE * ((lines[m] + 2) % SIDE)
        left = quarter_rows(g, m, first)
        for b in range(CHIPS):
            add_quarter(front, y, m, first, b, product(left, pt, b))
            for d in (1, 2, 3):
                write(2 * ((y + d) % CHIPS) + m, b)
    pltpu.make_async_copy(front, front, done).wait()


def shards(parent_front, generators, diagonal_blocks, coupling, block_map, valid_rows):
    banded = parent_front.reshape(8, BLK, CHIPS, 2, LANES).transpose(0, 1, 3, 2, 4).reshape(8, BLK, BANDS, 1, LANES)
    any_spec = pl.BlockSpec(memory_space=pl.ANY)
    vmem = pl.BlockSpec(memory_space=pltpu.VMEM)
    bf16 = jnp.bfloat16
    front_shape = pltpu.VMEM((8, BANDS, BLK, LANES), jnp.float32)
    front, g, pt = pl.pallas_call(
        gather_kernel,
        name="gather",
        in_specs=[any_spec] * 6,
        out_specs=[vmem] * 3,
        out_shape=[
            front_shape,
            pltpu.VMEM((2, STRIPS, CHIPS, 2, STRIP, BLK), bf16),
            pltpu.VMEM((CHIPS, 2, BLK, BLK), bf16),
        ],
        scratch_shapes=[
            pltpu.SMEM(block_map.shape, jnp.int32),
            pltpu.SMEM(valid_rows.shape, jnp.int32),
            pltpu.VMEM((2, CHIPS, 2, BLK, BLK), bf16),
            pltpu.VMEM((2, GROUP, STRIP, BLK), bf16),
            pltpu.VMEM((GROUP, BLK, BLK), bf16),
            pltpu.VMEM((GROUP, BLK, BLK), bf16),
            pltpu.VMEM((2, BLK, BLK), bf16),
            pltpu.VMEM((2, 6, STRIP, BLK), bf16),
            pltpu.VMEM((2, STRIPS, STRIP, BLK), bf16),
            pltpu.SemaphoreType.DMA((7,)),
            pltpu.SemaphoreType.DMA,
            pltpu.SemaphoreType.DMA((len(GROUPS),)),
        ],
        compiler_params=pltpu.CompilerParams(
            collective_id=0, has_side_effects=True, vmem_limit_bytes=52 << 20
        ),
    )(block_map, valid_rows, generators, diagonal_blocks, coupling, banded)
    out, _ = pl.pallas_call(
        write_kernel,
        name="write",
        in_specs=[vmem] * 3,
        out_specs=[any_spec, vmem],
        out_shape=[jax.ShapeDtypeStruct((8, BLK, BANDS, 1, LANES), jnp.float32), front_shape],
        input_output_aliases={0: 1},
        scratch_shapes=[pltpu.SemaphoreType.DMA],
        compiler_params=pltpu.CompilerParams(vmem_limit_bytes=2 << 20),
    )(front, g, pt)
    return out.reshape(8, BLK, 2, CHIPS, LANES).transpose(0, 1, 3, 2, 4).reshape(8, BLK, CHIPS, BLK)


def solution(mesh):
    in_specs = (
        P(None, "row", None, "col"),
        P("row", None, None),
        P("row", None, None),
        P(),
        P(),
        P(),
    )
    out_specs = P(None, "row", None, "col")
    return jax.shard_map(shards, mesh=mesh, in_specs=in_specs, out_specs=out_specs, check_vma=False)
```

time: 34.4 us -> 29.4 us (0.85)
  Pallas kernels: 34.3 us -> 29.3 us
    pallas_call x2, Pallas kernels: 34.3 us -> 29.3 us  [the longest x1 26 us: shards(): pl.pallas_call(gather_kernel, name='gather', in_specs=[any_spec] * 6, out...]
where the time goes in v4:
time: 29.4 us; the launch traced here: 29.3 us
  Pallas kernels  29.3 us (100%)
    pallas_call x1, Pallas kernels, shards(): pl.pallas_call(gather_kernel, name='gather', in_specs=[any_spec] * 6, out...  26 us
    pallas_call x1, Pallas kernels, shards(): pl.pallas_call(write_kernel, name='write', in_specs=[vmem] * 3, out_specs...  3.32 us

profile of v4, /device:TPU:0, one launch (start us, length us, event | category | flops | bytes accessed | tf_op | source)
XLA Modules:
  0.0 29.3 jit_solution(11992471948788237582)
XLA Ops:
  0.0 26.0 %gather.1 = (f32[8,8,256,128]{3,2,1,0:T(8,128)S(1)}, bf16[2,16,4,2,16,256]{5,4,3,2,1,0:T(8,128)(2,1)S(1)}, bf16[4,2,256,256]{3,2,1,0:T(8,128)(2,1)S(1)}) custom-call(s32[2,48]{1,0:T(2,128)} %maps.1, s32[2,48]{1,0:T(2,128)} %counts.1, bf16[12,256,256]{2,1,0:T(8,128)(2,1)} %gen.1, bf16[12,256,256]{2,1,0:T(8,128)(2,1)} %diag.1, bf16[2,256,256]{2,1,0:T(8,128)(2,1)} %coup.1, ...), custom_call_target="tpu_custom_call" | custom-call | tf_op jit(solution)/shard_map/gather/pallas_call | solution.py:359
  26.0 3.3 %write.1 = (f32[8,256,8,1,128]{4,3,2,1,0:T(1,128)}, f32[8,8,256,128]{3,2,1,0:T(8,128)S(1)}) custom-call(f32[8,8,256,128]{3,2,1,0:T(8,128)S(1)} %get-tuple-element.9.taken, bf16[2,16,4,2,16,256]{5,4,3,2,1,0:T(8,128)(2,1)S(1)} %get-tuple-element.10.g, bf16[4,2,256,256]{3,2,1,0:T(8,128)(2,1)S(1)} %get-tuple-element.11.pt), custom_call_target="tpu_custom_call", output_to_operand_aliasing={{1}: (0, {})} | custom-call | tf_op jit(solution)/shard_map/write/pallas_call | solution.py:387

commit v5 on v4

--- a/solution.py
+++ b/solution.py
@@ -22,11 +22,9 @@
 
 
 def arrival_groups():
-    names = ["S", "PR", "P0", "N0", "Q0", "P1"]
+    names = ["S", "SF", "PR", "P0", "N0", "Q0", "CL", "CO", "CF", "DX", "DD"]
     for m in range(2):
         names += [("A1", m), ("A2", m), ("B1", m, 0), ("B1", m, 1), ("B1", m, 2), ("B2", m)]
-    for part in range(2):
-        names += [("CL", part), ("CO", part), ("CF", part)]
     return {name: i for i, name in enumerate(names)}
 
 
@@ -57,7 +55,8 @@
 
 
 def gather_kernel(
-    maps, counts, gen, diag, coup, parent, front, g, pt, bmap, vrows, cd, gp, gv, dv, cw, sb, pb, lsem, ssem, rsem
+    maps, counts, gen, diag, coup, parent, front, g, pt,
+    bmap, vrows, cd, gp, gv, dv, cw, sb, sf, pb, dm, dx, dc, dd, lsem, ssem, dsem, rsem
 ):
     r = lax.axis_index("row")
     t = lax.axis_index("col")
@@ -82,7 +81,7 @@
 
     barrier = pltpu.get_barrier_semaphore()
     peers = [ydev(s, k) for s in (2, 1, 3) for k in range(CORES)] + [partner]
-    peers += [dev(m, s, 0) for s in (2, 1, -1) for m in range(2)]
+    peers += [dev(m, s, 0) for s in (1, -1) for m in range(2)]
     for peer in peers:
         pl.semaphore_signal(barrier, inc=1, device_id=peer, device_id_type=MESH)
 
@@ -127,19 +126,20 @@
 
     pl.semaphore_wait(barrier, len(peers))
 
-    sent = []
+    sent = [0, 0]
 
     def send(group, src, dst, to):
+        plane = int(isinstance(group, tuple))
         copy = pltpu.make_async_remote_copy(
-            src_ref=src, dst_ref=dst, send_sem=ssem, recv_sem=rsem.at[GROUPS[group]],
+            src_ref=src, dst_ref=dst, send_sem=ssem.at[plane], recv_sem=rsem.at[GROUPS[group]],
             device_id=to, device_id_type=MESH,
         )
         copy.start()
-        sent.append(math.prod(src.shape))
+        sent[plane] += math.prod(src.shape)
 
     def arrived(group, size):
         pltpu.make_async_remote_copy(
-            src_ref=size, dst_ref=size, send_sem=ssem, recv_sem=rsem.at[GROUPS[group]],
+            src_ref=size, dst_ref=size, send_sem=ssem.at[0], recv_sem=rsem.at[GROUPS[group]],
             device_id=partner, device_id_type=MESH,
         ).wait_recv()
 
@@ -150,7 +150,7 @@
                 send("S", sb.at[m, i], g.at[m, own_strip[m], d, c], ydev(-d, k))
     load_gen.wait()
     index, wanted = source(t)
-    cd[c, y, 0] = jnp.where(down < wanted, gv[index], zero)
+    cd[c, y] = jnp.where(down < wanted, gv[index], zero)
     for m in range(2):
         index, count = source(m * 8 + y * CORES + other)
         pb[m] = jnp.where(down < count, gv[index], zero).reshape(STRIPS, STRIP, BLK)
@@ -161,26 +161,29 @@
     def onward(d):
         return 0 if d == 1 else 1
 
-    def send_own(part, lead):
+    for lead in (True, False):
         for d in (1, -1):
-            k = onward(d) if lead else 1 - onward(d)
-            ref = cd.at[c, y, part, rows_of(k)]
-            send(("CL" if lead else "CO", part), ref, ref, ydev(d, c))
-
-    send_own(0, True)
-    send_own(0, False)
-    send("P0", cd.at[c, y, 0], cd.at[c, y, 0], partner)
+            half = cd.at[c, y, rows_of(onward(d) if lead else 1 - onward(d))]
+            send("CL" if lead else "CO", half, half, ydev(d, c))
+    send("P0", cd.at[c, y], cd.at[c, y], partner)
+    far_strip = [strip(0, 2, 2), strip(1, 2, 2)]
     for m in range(2):
         send("PR", pb.at[m], g.at[m, :, 0, c], partner)
         index, count = source(m * 8 + r)
         g[m, :, 0, c] = jnp.where(down < count, gv[index], zero).reshape(STRIPS, STRIP, BLK)
+        for d in (1, 2, 3):
+            for k in range(CORES):
+                index, count = source(m * 8 + CORES * wrap(y - d) + k)
+                inside = down[:STRIP] + far_strip[m] * STRIP < count
+                rows = gv[index, pl.ds(pl.multiple_of(far_strip[m] * STRIP, STRIP), STRIP)]
+                sf[m, (d - 1) * CORES + k] = jnp.where(inside, rows, zero)
     load_diag.wait()
     across = lax.broadcasted_iota(jnp.int32, (BLK, BLK), 1)
     index, count = source(t)
-    cd[c, y, 1] = jnp.where(jnp.logical_and(down < count, across < count), dv[index], zero)
+    dm[...] = jnp.where(jnp.logical_and(down < count, across < count), dv[index], zero)
     for load in load_front:
         load.start()
-    send_own(1, True)
+    send("DX", dm.at[pl.ds(other * HALF, HALF)], dx, partner)
     load_coup.wait()
     for child in range(2):
         cw[child] = cw[child].T
@@ -203,30 +206,12 @@
                 ref = piece(m, item, -d, onward(d))
                 send(("B2", m), ref, ref, dev(m, 0, d))
 
-    one_block = cd.at[0, 0, 0]
-
-    def relay(part):
-        arrived(("CL", part), one_block)
-        for d in (1, -1):
-            half = cd.at[c, wrap(y - d), part, rows_of(onward(d))]
-            send(("CF", part), half, half, ydev(d, c))
-
-    def near(part):
-        arrived(("CO", part), one_block)
-        for d in (1, -1):
-            ref = cd.at[c, wrap(y - d), part]
-            send(("N0", "P1")[part], ref, ref, partner)
-
-    def far(part):
-        arrived(("CF", part), one_block)
-        for d in (1, -1):
-            half = cd.at[c, wrap(y + 2), part, rows_of(onward(d))]
-            send(("Q0", "P1")[part], half, half, partner)
+    one_block = cd.at[0, 0]
 
     def project(s):
         for child in range(2):
             proj = lax.dot_general(
-                cw[child], cd[child, s, 0], (((1,), (1,)), ((), ())), preferred_element_type=jnp.float32
+                cw[child], cd[child, s], (((1,), (1,)), ((), ())), preferred_element_type=jnp.float32
             )
             pt[s, child] = proj.astype(jnp.bfloat16)
 
@@ -247,55 +232,75 @@
         for b in range(CHIPS):
             add_quarter(front, y, m, first, b, multiply(left, b))
 
-    def add_diagonals():
-        for b in range(CHIPS):
-            total = cd[0, b, 1].astype(jnp.float32) + cd[1, b, 1].astype(jnp.float32)
-            add_to(2 * b + t // 8, 0, BLK, b, total)
-
     arrived("P0", one_block)
     project(y)
+    arrived("DX", dx)
+    total = dm[pl.ds(c * HALF, HALF)].astype(jnp.float32) + dx[...].astype(jnp.float32)
+    dc[...] = total.astype(jnp.bfloat16)
     arrived("PR", g.at[:, :, 0, 0])
+
+    def diagonal_send():
+        return pltpu.make_async_remote_copy(
+            src_ref=dc, dst_ref=dd.at[y, pl.ds(c * HALF, HALF)], send_sem=dsem, recv_sem=rsem.at[GROUPS["DD"]],
+            device_id=(t % 8, t), device_id_type=MESH,
+        )
+
     arrived("S", g.at[0, pl.ds(0, 2), pl.ds(1, 3)])
     for m in range(2):
         ref = piece(m, 0, 0)
         for d in (1, -1):
             send(("A1", m), ref, ref, dev(m, d, 0))
-        send(("A2", m), ref, ref, dev(m, 2, 0))
     for m in range(2):
         first_q(m, 0)
-    send("P1", cd.at[c, y, 1], cd.at[c, y, 1], partner)
-    relay(0)
-    send_own(1, False)
+    arrived("CL", one_block)
+    for d in (1, -1):
+        half = cd.at[c, wrap(y - d), rows_of(onward(d))]
+        send("CF", half, half, ydev(d, c))
+    for d in (2, 1, 3):
+        for m in range(2):
+            for k in range(CORES):
+                send("SF", sf.at[m, (d - 1) * CORES + k], g.at[m, far_strip[m], d, c], ydev(-d, k))
+
+    @pl.when(r != t % 8)
+    def _():
+        diagonal_send().start()
+
     pltpu.make_async_copy(front, front, lsem.at[6]).wait()
     own_tiles(y)
-    near(0)
+    arrived("CO", one_block)
+    for d in (1, -1):
+        ref = cd.at[c, wrap(y - d)]
+        send("N0", ref, ref, partner)
     for m in range(2):
         arrived(("A1", m), g.at[m, pl.ds(0, 2), pl.ds(1, 3)])
         for d in (1, -1):
-            first_q(m, -d)
+            ref = piece(m, -d, 0, onward(d))
+            send(("A2", m), ref, ref, dev(m, d, 0))
+    for m in range(2):
+        for d in (1, -1):
+            first_q(m, d)
     for m in range(2):
         second_q(m, (0,))
-    far(0)
-    for m in range(2):
-        arrived(("A2", m), g.at[m, 0, pl.ds(1, 3)])
-        first_q(m, 2)
-    relay(1)
-    near(1)
-    arrived("N0", cd.at[0, pl.ds(0, 2), 0])
+    arrived("N0", cd.at[0, pl.ds(0, 2)])
 
     @pl.loop(0, 2)
     def _(i):
         project(wrap(y + 2 * i - 1))
 
-    for m in range(2):
-        second_q(m, (1, -1))
+    arrived("CF", one_block)
+    for d in (1, -1):
+        half = cd.at[c, wrap(y + 2), rows_of(onward(d))]
+        send("Q0", half, half, partner)
+    for m in range(2):
+        arrived(("A2", m), g.at[m, 0, pl.ds(1, 3)])
+        first_q(m, 2)
 
     @pl.loop(0, 2)
     def _(i):
         own_tiles(wrap(y + 2 * i - 1))
 
     for m in range(2):
-        second_q(m, (2,))
+        second_q(m, (1, -1))
     arrived("Q0", one_block)
     project(wrap(y + 2))
     own_tiles(wrap(y + 2))
@@ -304,27 +309,30 @@
     def _(m):
         quarter(m, 0)
 
-    far(1)
-
-    @pl.loop(0, 4)
-    def _(i):
-        quarter(i // 2, 2 * (i % 2) - 1)
-
-    arrived("P1", cd.at[0, :, 1])
-
     @pl.when(r == t % 8)
     def _():
-        add_diagonals()
-
-    for m in range(2):
-        arrived(("B2", m), g.at[m, pl.ds(0, 4), pl.ds(1, 3)])
-    blocks, rest = divmod(sum(sent), 2 * CHIPS * BLK * LANES)
-    assert rest == 0
-    everything = front.at[pl.ds(0, blocks), pl.ds(0, CHIPS)]
-    pltpu.make_async_remote_copy(
-        src_ref=everything, dst_ref=everything, send_sem=ssem, recv_sem=rsem.at[0],
-        device_id=partner, device_id_type=MESH,
-    ).wait_send()
+        dd[y, pl.ds(c * HALF, HALF)] = dc[...]
+        arrived("DD", gv.at[pl.ds(0, 7), pl.ds(0, HALF)])
+        for b in range(CHIPS):
+            add_to(2 * b + t // 8, 0, BLK, b, dd[b].astype(jnp.float32))
+
+    @pl.when(r != t % 8)
+    def _():
+        diagonal_send().wait_send()
+
+    for m in range(2):
+        arrived(("B1", m, 2), g.at[m, pl.ds(0, 2), pl.ds(1, 3)])
+    arrived("SF", g.at[0, pl.ds(0, 2), pl.ds(1, 3)])
+    for m in range(2):
+        arrived(("B2", m), g.at[m, pl.ds(0, 3), pl.ds(1, 3)])
+    for plane in range(2):
+        rows, rest = divmod(sent[plane], 2 * 2 * BANDS * LANES)
+        assert rest == 0 and rows <= BLK and rows % 8 == 0
+        size = front.at[pl.ds(0, 2), :, pl.ds(0, rows)]
+        pltpu.make_async_remote_copy(
+            src_ref=size, dst_ref=size, send_sem=ssem.at[plane], recv_sem=rsem.at[0],
+            device_id=partner, device_id_type=MESH,
+        ).wait_send()
 
 
 def write_kernel(taken, g, pt, out, front, done):
@@ -341,10 +349,11 @@
         for b in range(CHIPS):
             write(2 * y + m, b)
     for m in range(2):
-        first = SIDE * ((lines[m] + 2) % SIDE)
-        left = quarter_rows(g, m, first)
+        firsts = [SIDE * ((lines[m] + step) % SIDE) for step in (1, 3, 2)]
+        lefts = [quarter_rows(g, m, first) for first in firsts]
         for b in range(CHIPS):
-            add_quarter(front, y, m, first, b, product(left, pt, b))
+            for first, left in zip(firsts, lefts):
+                add_quarter(front, y, m, first, b, product(left, pt, b))
             for d in (1, 2, 3):
                 write(2 * ((y + d) % CHIPS) + m, b)
     pltpu.make_async_copy(front, front, done).wait()
@@ -369,14 +378,20 @@
         scratch_shapes=[
             pltpu.SMEM(block_map.shape, jnp.int32),
             pltpu.SMEM(valid_rows.shape, jnp.int32),
-            pltpu.VMEM((2, CHIPS, 2, BLK, BLK), bf16),
+            pltpu.VMEM((2, CHIPS, BLK, BLK), bf16),
             pltpu.VMEM((2, GROUP, STRIP, BLK), bf16),
             pltpu.VMEM((GROUP, BLK, BLK), bf16),
             pltpu.VMEM((GROUP, BLK, BLK), bf16),
             pltpu.VMEM((2, BLK, BLK), bf16),
             pltpu.VMEM((2, 6, STRIP, BLK), bf16),
+            pltpu.VMEM((2, 6, STRIP, BLK), bf16),
             pltpu.VMEM((2, STRIPS, STRIP, BLK), bf16),
+            pltpu.VMEM((BLK, BLK), bf16),
+            pltpu.VMEM((HALF, BLK), bf16),
+            pltpu.VMEM((HALF, BLK), bf16),
+            pltpu.VMEM((CHIPS, BLK, BLK), bf16),
             pltpu.SemaphoreType.DMA((7,)),
+            pltpu.SemaphoreType.DMA((2,)),
             pltpu.SemaphoreType.DMA,
             pltpu.SemaphoreType.DMA((len(GROUPS),)),
         ],

time: 29.4 us -> 27.2 us (0.925)
  Pallas kernels: 29.3 us -> 27.1 us
    pallas_call x1, Pallas kernels: 26 us -> 23.9 us  [shards(): pl.pallas_call(gather_kernel, name='gather', in_specs=[any_spec] * 6, out...]
where the time goes in v5:
time: 27.2 us; the launch traced here: 27.1 us
  Pallas kernels  27.1 us (100%)
    pallas_call x1, Pallas kernels, shards(): pl.pallas_call(gather_kernel, name='gather', in_specs=[any_spec] * 6, out...  23.9 us
    pallas_call x1, Pallas kernels, shards(): pl.pallas_call(write_kernel, name='write', in_specs=[vmem] * 3, out_specs...  3.27 us

profile of v5, /device:TPU:0, one launch (start us, length us, event | category | flops | bytes accessed | tf_op | source)
XLA Modules:
  0.0 27.1 jit_solution(15456000716957766340)
XLA Ops:
  0.0 23.9 %gather.1 = (f32[8,8,256,128]{3,2,1,0:T(8,128)S(1)}, bf16[2,16,4,2,16,256]{5,4,3,2,1,0:T(8,128)(2,1)S(1)}, bf16[4,2,256,256]{3,2,1,0:T(8,128)(2,1)S(1)}) custom-call(s32[2,48]{1,0:T(2,128)} %maps.1, s32[2,48]{1,0:T(2,128)} %counts.1, bf16[12,256,256]{2,1,0:T(8,128)(2,1)} %gen.1, bf16[12,256,256]{2,1,0:T(8,128)(2,1)} %diag.1, bf16[2,256,256]{2,1,0:T(8,128)(2,1)} %coup.1, ...), custom_call_target="tpu_custom_call" | custom-call | tf_op jit(solution)/shard_map/gather/pallas_call | solution.py:368
  23.9 3.3 %write.1 = (f32[8,256,8,1,128]{4,3,2,1,0:T(1,128)}, f32[8,8,256,128]{3,2,1,0:T(8,128)S(1)}) custom-call(f32[8,8,256,128]{3,2,1,0:T(8,128)S(1)} %get-tuple-element.9.taken, bf16[2,16,4,2,16,256]{5,4,3,2,1,0:T(8,128)(2,1)S(1)} %get-tuple-element.10.g, bf16[4,2,256,256]{3,2,1,0:T(8,128)(2,1)S(1)} %get-tuple-element.11.pt), custom_call_target="tpu_custom_call", output_to_operand_aliasing={{1}: (0, {})} | custom-call | tf_op jit(solution)/shard_map/write/pallas_call | solution.py:402

commit v6 on v5

--- a/solution.py
+++ b/solution.py
@@ -24,7 +24,7 @@
 def arrival_groups():
     names = ["S", "SF", "PR", "P0", "N0", "Q0", "CL", "CO", "CF", "DX", "DD"]
     for m in range(2):
-        names += [("A1", m), ("A2", m), ("B1", m, 0), ("B1", m, 1), ("B1", m, 2), ("B2", m)]
+        names += [("A1", m), ("A2", m), ("B1", m, 0), ("B1", m, 1), ("B1", m, 2), ("B2", m), ("A1r", m), ("B1r", m)]
     return {name: i for i, name in enumerate(names)}
 
 
@@ -200,7 +200,7 @@
             send(("B1", m, abs(item)), ref, ref, dev(m, 0, d))
 
     def second_q(m, items):
-        arrived(("B1", m, abs(items[0])), g.at[m, pl.ds(0, 2 * len(items)), pl.ds(1, 3)])
+        arrived(("B1", m, abs(items[0])), g.at[m, pl.ds(0, 2), pl.ds(1, 3)])
         for item in items:
             for d in (1, -1):
                 ref = piece(m, item, -d, onward(d))
@@ -246,10 +246,11 @@
         )
 
     arrived("S", g.at[0, pl.ds(0, 2), pl.ds(1, 3)])
-    for m in range(2):
-        ref = piece(m, 0, 0)
-        for d in (1, -1):
-            send(("A1", m), ref, ref, dev(m, d, 0))
+    for lead in (True, False):
+        for m in range(2):
+            for d in (1, -1):
+                ref = piece(m, 0, 0, onward(d) if lead else 1 - onward(d))
+                send(("A1" if lead else "A1r", m), ref, ref, dev(m, d, 0))
     for m in range(2):
         first_q(m, 0)
     arrived("CL", one_block)
@@ -272,13 +273,24 @@
         ref = cd.at[c, wrap(y - d)]
         send("N0", ref, ref, partner)
     for m in range(2):
-        arrived(("A1", m), g.at[m, pl.ds(0, 2), pl.ds(1, 3)])
+        arrived(("A1", m), g.at[m, 0, pl.ds(1, 3)])
         for d in (1, -1):
             ref = piece(m, -d, 0, onward(d))
             send(("A2", m), ref, ref, dev(m, d, 0))
     for m in range(2):
         for d in (1, -1):
-            first_q(m, d)
+            ref = piece(m, -d, 0, onward(d))
+            send(("B1", m, 1), ref, ref, dev(m, 0, d))
+    for m in range(2):
+        arrived(("A1r", m), g.at[m, 0, pl.ds(1, 3)])
+        for d in (1, -1):
+            ref = piece(m, d, 0, onward(d))
+            send(("B1", m, 1), ref, ref, dev(m, 0, d))
+    for m in range(2):
+        for d in (1, -1):
+            for item in (1, -1):
+                ref = piece(m, item, 0, 1 - onward(d))
+                send(("B1r", m), ref, ref, dev(m, 0, d))
     for m in range(2):
         second_q(m, (0,))
     arrived("N0", cd.at[0, pl.ds(0, 2)])
@@ -287,20 +299,21 @@
     def _(i):
         project(wrap(y + 2 * i - 1))
 
+    for m in range(2):
+        arrived(("A2", m), g.at[m, 0, pl.ds(1, 3)])
+        first_q(m, 2)
     arrived("CF", one_block)
     for d in (1, -1):
         half = cd.at[c, wrap(y + 2), rows_of(onward(d))]
         send("Q0", half, half, partner)
-    for m in range(2):
-        arrived(("A2", m), g.at[m, 0, pl.ds(1, 3)])
-        first_q(m, 2)
+
+    for m in range(2):
+        second_q(m, (1, -1))
 
     @pl.loop(0, 2)
     def _(i):
         own_tiles(wrap(y + 2 * i - 1))
 
-    for m in range(2):
-        second_q(m, (1, -1))
     arrived("Q0", one_block)
     project(wrap(y + 2))
     own_tiles(wrap(y + 2))
@@ -321,6 +334,7 @@
         diagonal_send().wait_send()
 
     for m in range(2):
+        arrived(("B1r", m), g.at[m, pl.ds(0, 2), pl.ds(1, 3)])
         arrived(("B1", m, 2), g.at[m, pl.ds(0, 2), pl.ds(1, 3)])
     arrived("SF", g.at[0, pl.ds(0, 2), pl.ds(1, 3)])
     for m in range(2):

time: 27.2 us -> 26.2 us (0.963)
  Pallas kernels: 27.1 us -> 26.1 us
    pallas_call x1, Pallas kernels: 23.9 us -> 22.8 us  [shards(): pl.pallas_call(gather_kernel, name='gather', in_specs=[any_spec] * 6, out...]
where the time goes in v6:
time: 26.2 us; the launch traced here: 26.1 us
  Pallas kernels  26.1 us (100%)
    pallas_call x1, Pallas kernels, shards(): pl.pallas_call(gather_kernel, name='gather', in_specs=[any_spec] * 6, out...  22.8 us
    pallas_call x1, Pallas kernels, shards(): pl.pallas_call(write_kernel, name='write', in_specs=[vmem] * 3, out_specs...  3.27 us

profile of v6, /device:TPU:0, one launch (start us, length us, event | category | flops | bytes accessed | tf_op | source)
XLA Modules:
  0.0 26.1 jit_solution(2081386190871704650)
XLA Ops:
  0.0 22.8 %gather.1 = (f32[8,8,256,128]{3,2,1,0:T(8,128)S(1)}, bf16[2,16,4,2,16,256]{5,4,3,2,1,0:T(8,128)(2,1)S(1)}, bf16[4,2,256,256]{3,2,1,0:T(8,128)(2,1)S(1)}) custom-call(s32[2,48]{1,0:T(2,128)} %maps.1, s32[2,48]{1,0:T(2,128)} %counts.1, bf16[12,256,256]{2,1,0:T(8,128)(2,1)} %gen.1, bf16[12,256,256]{2,1,0:T(8,128)(2,1)} %diag.1, bf16[2,256,256]{2,1,0:T(8,128)(2,1)} %coup.1, ...), custom_call_target="tpu_custom_call" | custom-call | tf_op jit(solution)/shard_map/gather/pallas_call | solution.py:382
  22.8 3.3 %write.1 = (f32[8,256,8,1,128]{4,3,2,1,0:T(1,128)}, f32[8,8,256,128]{3,2,1,0:T(8,128)S(1)}) custom-call(f32[8,8,256,128]{3,2,1,0:T(8,128)S(1)} %get-tuple-element.9.taken, bf16[2,16,4,2,16,256]{5,4,3,2,1,0:T(8,128)(2,1)S(1)} %get-tuple-element.10.g, bf16[4,2,256,256]{3,2,1,0:T(8,128)(2,1)S(1)} %get-tuple-element.11.pt), custom_call_target="tpu_custom_call", output_to_operand_aliasing={{1}: (0, {})} | custom-call | tf_op jit(solution)/shard_map/write/pallas_call | solution.py:416

commit v7 on v6

--- a/solution.py
+++ b/solution.py
@@ -22,9 +22,9 @@
 
 
 def arrival_groups():
-    names = ["S", "SF", "PR", "P0", "N0", "Q0", "CL", "CO", "CF", "DX", "DD"]
-    for m in range(2):
-        names += [("A1", m), ("A2", m), ("B1", m, 0), ("B1", m, 1), ("B1", m, 2), ("B2", m), ("A1r", m), ("B1r", m)]
+    names = ["S", "end", "PR", "P0", "N0", "Q0", "CL", "CO", "CF", "DX", "DD"]
+    for m in range(2):
+        names += [("A1", m), ("A2", m), ("B1", m, 0), ("B1", m, 1), ("A1r", m)]
     return {name: i for i, name in enumerate(names)}
 
 
@@ -129,7 +129,7 @@
     sent = [0, 0]
 
     def send(group, src, dst, to):
-        plane = int(isinstance(group, tuple))
+        plane = int(to[0] is r)
         copy = pltpu.make_async_remote_copy(
             src_ref=src, dst_ref=dst, send_sem=ssem.at[plane], recv_sem=rsem.at[GROUPS[group]],
             device_id=to, device_id_type=MESH,
@@ -194,17 +194,16 @@
             return g.at[m, at, pl.ds(1, 3)]
         return g.at[m, at, pl.ds(1, 3), part]
 
-    def first_q(m, item):
-        for d in (1, -1):
-            ref = piece(m, item, 0)
-            send(("B1", m, abs(item)), ref, ref, dev(m, 0, d))
+    def first_q(m, item, child, group, d):
+        ref = piece(m, item, 0, child)
+        send(group, ref, ref, dev(m, 0, d))
 
     def second_q(m, items):
-        arrived(("B1", m, abs(items[0])), g.at[m, pl.ds(0, 2), pl.ds(1, 3)])
+        arrived(("B1", m, abs(items[0])), g.at[m, pl.ds(0, len(items)), pl.ds(1, 3)])
         for item in items:
             for d in (1, -1):
                 ref = piece(m, item, -d, onward(d))
-                send(("B2", m), ref, ref, dev(m, 0, d))
+                send("end", ref, ref, dev(m, 0, d))
 
     one_block = cd.at[0, 0]
 
@@ -252,7 +251,11 @@
                 ref = piece(m, 0, 0, onward(d) if lead else 1 - onward(d))
                 send(("A1" if lead else "A1r", m), ref, ref, dev(m, d, 0))
     for m in range(2):
-        first_q(m, 0)
+        for d in (1, -1):
+            first_q(m, 0, onward(d), ("B1", m, 0), d)
+    for m in range(2):
+        for d in (1, -1):
+            first_q(m, 0, 1 - onward(d), "end", d)
     arrived("CL", one_block)
     for d in (1, -1):
         half = cd.at[c, wrap(y - d), rows_of(onward(d))]
@@ -260,7 +263,7 @@
     for d in (2, 1, 3):
         for m in range(2):
             for k in range(CORES):
-                send("SF", sf.at[m, (d - 1) * CORES + k], g.at[m, far_strip[m], d, c], ydev(-d, k))
+                send("end", sf.at[m, (d - 1) * CORES + k], g.at[m, far_strip[m], d, c], ydev(-d, k))
 
     @pl.when(r != t % 8)
     def _():
@@ -268,30 +271,30 @@
 
     pltpu.make_async_copy(front, front, lsem.at[6]).wait()
     own_tiles(y)
+    for m in range(2):
+        arrived(("A1", m), g.at[m, 0, pl.ds(1, 3)])
+        for d in (1, -1):
+            ref = piece(m, -d, 0, onward(d))
+            send(("A2", m), ref, ref, dev(m, d, 0))
+    for m in range(2):
+        for d in (1, -1):
+            ref = piece(m, -d, 0, onward(d))
+            send(("B1", m, 1), ref, ref, dev(m, 0, d))
+    for m in range(2):
+        arrived(("A1r", m), g.at[m, 0, pl.ds(1, 3)])
+        for d in (1, -1):
+            ref = piece(m, d, 0, onward(d))
+            send(("B1", m, 1), ref, ref, dev(m, 0, d))
+    for m in range(2):
+        for d in (1, -1):
+            for item in (1, -1):
+                ref = piece(m, item, 0, 1 - onward(d))
+                send("end", ref, ref, dev(m, 0, d))
     arrived("CO", one_block)
     for d in (1, -1):
         ref = cd.at[c, wrap(y - d)]
         send("N0", ref, ref, partner)
     for m in range(2):
-        arrived(("A1", m), g.at[m, 0, pl.ds(1, 3)])
-        for d in (1, -1):
-            ref = piece(m, -d, 0, onward(d))
-            send(("A2", m), ref, ref, dev(m, d, 0))
-    for m in range(2):
-        for d in (1, -1):
-            ref = piece(m, -d, 0, onward(d))
-            send(("B1", m, 1), ref, ref, dev(m, 0, d))
-    for m in range(2):
-        arrived(("A1r", m), g.at[m, 0, pl.ds(1, 3)])
-        for d in (1, -1):
-            ref = piece(m, d, 0, onward(d))
-            send(("B1", m, 1), ref, ref, dev(m, 0, d))
-    for m in range(2):
-        for d in (1, -1):
-            for item in (1, -1):
-                ref = piece(m, item, 0, 1 - onward(d))
-                send(("B1r", m), ref, ref, dev(m, 0, d))
-    for m in range(2):
         second_q(m, (0,))
     arrived("N0", cd.at[0, pl.ds(0, 2)])
 
@@ -301,7 +304,8 @@
 
     for m in range(2):
         arrived(("A2", m), g.at[m, 0, pl.ds(1, 3)])
-        first_q(m, 2)
+        for d in (1, -1):
+            first_q(m, 2, None, "end", d)
     arrived("CF", one_block)
     for d in (1, -1):
         half = cd.at[c, wrap(y + 2), rows_of(onward(d))]
@@ -333,12 +337,7 @@
     def _():
         diagonal_send().wait_send()
 
-    for m in range(2):
-        arrived(("B1r", m), g.at[m, pl.ds(0, 2), pl.ds(1, 3)])
-        arrived(("B1", m, 2), g.at[m, pl.ds(0, 2), pl.ds(1, 3)])
-    arrived("SF", g.at[0, pl.ds(0, 2), pl.ds(1, 3)])
-    for m in range(2):
-        arrived(("B2", m), g.at[m, pl.ds(0, 3), pl.ds(1, 3)])
+    arrived("end", g.at[:, pl.ds(0, 9), pl.ds(1, 3)])
     for plane in range(2):
         rows, rest = divmod(sent[plane], 2 * 2 * BANDS * LANES)
         assert rest == 0 and rows <= BLK and rows % 8 == 0

time: 26.2 us -> 25.9 us (0.989)
  Pallas kernels: 26.1 us -> 25.7 us
    pallas_call x1, Pallas kernels: 22.8 us -> 22.5 us  [shards(): pl.pallas_call(gather_kernel, name='gather', in_specs=[any_spec] * 6, out...]
where the time goes in v7:
time: 25.9 us; the launch traced here: 25.8 us
  Pallas kernels  25.7 us (99%)
    pallas_call x1, Pallas kernels, shards(): pl.pallas_call(gather_kernel, name='gather', in_specs=[any_spec] * 6, out...  22.5 us
    pallas_call x1, Pallas kernels, shards(): pl.pallas_call(write_kernel, name='write', in_specs=[vmem] * 3, out_specs...  3.27 us

profile of v7, /device:TPU:0, one launch (start us, length us, event | category | flops | bytes accessed | tf_op | source)
XLA Modules:
  0.0 25.8 jit_solution(17226548802027320212)
XLA Ops:
  0.0 22.5 %gather.1 = (f32[8,8,256,128]{3,2,1,0:T(8,128)S(1)}, bf16[2,16,4,2,16,256]{5,4,3,2,1,0:T(8,128)(2,1)S(1)}, bf16[4,2,256,256]{3,2,1,0:T(8,128)(2,1)S(1)}) custom-call(s32[2,48]{1,0:T(2,128)} %maps.1, s32[2,48]{1,0:T(2,128)} %counts.1, bf16[12,256,256]{2,1,0:T(8,128)(2,1)} %gen.1, bf16[12,256,256]{2,1,0:T(8,128)(2,1)} %diag.1, bf16[2,256,256]{2,1,0:T(8,128)(2,1)} %coup.1, ...), custom_call_target="tpu_custom_call" | custom-call | tf_op jit(solution)/shard_map/gather/pallas_call | solution.py:381
  22.5 3.3 %write.1 = (f32[8,256,8,1,128]{4,3,2,1,0:T(1,128)}, f32[8,8,256,128]{3,2,1,0:T(8,128)S(1)}) custom-call(f32[8,8,256,128]{3,2,1,0:T(8,128)S(1)} %get-tuple-element.9.taken, bf16[2,16,4,2,16,256]{5,4,3,2,1,0:T(8,128)(2,1)S(1)} %get-tuple-element.10.g, bf16[4,2,256,256]{3,2,1,0:T(8,128)(2,1)S(1)} %get-tuple-element.11.pt), custom_call_target="tpu_custom_call", output_to_operand_aliasing={{1}: (0, {})} | custom-call | tf_op jit(solution)/shard_map/write/pallas_call | solution.py:415

commit v8 on v7

--- a/solution.py
+++ b/solution.py
@@ -260,6 +260,27 @@
     for d in (1, -1):
         half = cd.at[c, wrap(y - d), rows_of(onward(d))]
         send("CF", half, half, ydev(d, c))
+    pltpu.make_async_copy(front, front, lsem.at[6]).wait()
+    own_tiles(y)
+    for m in range(2):
+        arrived(("A1", m), g.at[m, 0, pl.ds(1, 3)])
+        for d in (1, -1):
+            ref = piece(m, -d, 0, onward(d))
+            send(("A2", m), ref, ref, dev(m, d, 0))
+    for m in range(2):
+        for d in (1, -1):
+            ref = piece(m, -d, 0, onward(d))
+            send(("B1", m, 1), ref, ref, dev(m, 0, d))
+    for m in range(2):
+        arrived(("A1r", m), g.at[m, 0, pl.ds(1, 3)])
+        for d in (1, -1):
+            ref = piece(m, d, 0, onward(d))
+            send(("B1", m, 1), ref, ref, dev(m, 0, d))
+    for m in range(2):
+        for d in (1, -1):
+            for item in (1, -1):
+                ref = piece(m, item, 0, 1 - onward(d))
+                send("end", ref, ref, dev(m, 0, d))
     for d in (2, 1, 3):
         for m in range(2):
             for k in range(CORES):
@@ -269,39 +290,18 @@
     def _():
         diagonal_send().start()
 
-    pltpu.make_async_copy(front, front, lsem.at[6]).wait()
-    own_tiles(y)
-    for m in range(2):
-        arrived(("A1", m), g.at[m, 0, pl.ds(1, 3)])
-        for d in (1, -1):
-            ref = piece(m, -d, 0, onward(d))
-            send(("A2", m), ref, ref, dev(m, d, 0))
-    for m in range(2):
-        for d in (1, -1):
-            ref = piece(m, -d, 0, onward(d))
-            send(("B1", m, 1), ref, ref, dev(m, 0, d))
-    for m in range(2):
-        arrived(("A1r", m), g.at[m, 0, pl.ds(1, 3)])
-        for d in (1, -1):
-            ref = piece(m, d, 0, onward(d))
-            send(("B1", m, 1), ref, ref, dev(m, 0, d))
-    for m in range(2):
-        for d in (1, -1):
-            for item in (1, -1):
-                ref = piece(m, item, 0, 1 - onward(d))
-                send("end", ref, ref, dev(m, 0, d))
     arrived("CO", one_block)
     for d in (1, -1):
         ref = cd.at[c, wrap(y - d)]
         send("N0", ref, ref, partner)
-    for m in range(2):
-        second_q(m, (0,))
     arrived("N0", cd.at[0, pl.ds(0, 2)])
 
     @pl.loop(0, 2)
     def _(i):
         project(wrap(y + 2 * i - 1))
 
+    for m in range(2):
+        second_q(m, (0,))
     for m in range(2):
         arrived(("A2", m), g.at[m, 0, pl.ds(1, 3)])
         for d in (1, -1):

time: 25.9 us -> 25.7 us (level)
  no operation moved by 1% of the time
where the time goes in v8:
time: 25.7 us; the launch traced here: 25.6 us
  Pallas kernels  25.6 us (100%)
    pallas_call x1, Pallas kernels, shards(): pl.pallas_call(gather_kernel, name='gather', in_specs=[any_spec] * 6, out...  22.3 us
    pallas_call x1, Pallas kernels, shards(): pl.pallas_call(write_kernel, name='write', in_specs=[vmem] * 3, out_specs...  3.27 us

profile of v8, /device:TPU:0, one launch (start us, length us, event | category | flops | bytes accessed | tf_op | source)
XLA Modules:
  0.0 25.6 jit_solution(5338985468471628329)
XLA Ops:
  0.0 22.3 %gather.1 = (f32[8,8,256,128]{3,2,1,0:T(8,128)S(1)}, bf16[2,16,4,2,16,256]{5,4,3,2,1,0:T(8,128)(2,1)S(1)}, bf16[4,2,256,256]{3,2,1,0:T(8,128)(2,1)S(1)}) custom-call(s32[2,48]{1,0:T(2,128)} %maps.1, s32[2,48]{1,0:T(2,128)} %counts.1, bf16[12,256,256]{2,1,0:T(8,128)(2,1)} %gen.1, bf16[12,256,256]{2,1,0:T(8,128)(2,1)} %diag.1, bf16[2,256,256]{2,1,0:T(8,128)(2,1)} %coup.1, ...), custom_call_target="tpu_custom_call" | custom-call | tf_op jit(solution)/shard_map/gather/pallas_call | solution.py:381
  22.3 3.3 %write.1 = (f32[8,256,8,1,128]{4,3,2,1,0:T(1,128)}, f32[8,8,256,128]{3,2,1,0:T(8,128)S(1)}) custom-call(f32[8,8,256,128]{3,2,1,0:T(8,128)S(1)} %get-tuple-element.9.taken, bf16[2,16,4,2,16,256]{5,4,3,2,1,0:T(8,128)(2,1)S(1)} %get-tuple-element.10.g, bf16[4,2,256,256]{3,2,1,0:T(8,128)(2,1)S(1)} %get-tuple-element.11.pt), custom_call_target="tpu_custom_call", output_to_operand_aliasing={{1}: (0, {})} | custom-call | tf_op jit(solution)/shard_map/write/pallas_call | solution.py:415
